TPU v7x, 8 devices: a whole 2x2x1 slice. The times are simulated.
8 devices in a mesh: dp: 1 (over z), wg: 8 (over y, x, core).
Axes of the slice: x: 2, y: 2, z: 1, core: 2. Of those that a mesh axis runs over, the one named last changes fastest.
Arguments:
- x: bfloat16 [8, 256, 2560], P(('dp', 'wg'))
- positions: int32 [256], P('dp')
- prompt_len: int32 [8], P(('dp', 'wg'))
- ln_attn: bfloat16 [2, 2, 2560], P(None, None, 'wg')
- ln_mlp: bfloat16 [2, 2, 2560], P(None, None, 'wg')
- w_qkv: bfloat16 [2, 2560, 7680], P(None, None, 'wg')
- w_out: bfloat16 [2, 32, 80, 2560], P(None, None, None, 'wg')
- w_up: bfloat16 [2, 2560, 10240], P(None, None, 'wg')
- w_down: bfloat16 [2, 10240, 2560], P(None, None, 'wg')
Outputs:
- output 1: bfloat16 [8, 256, 2560], P(('dp', 'wg'))
- output 2: bfloat16 [2, 8, 256, 32, 80], P(None, ('dp', 'wg'))
- output 3: bfloat16 [2, 8, 256, 32, 80], P(None, ('dp', 'wg'))
All inputs are finite; a program needn't handle non-finite values.
Results may differ from a plain program's by a relative error of at most 0.0144262.
Values are sent between devices in bfloat16 or wider.
A program may use at most 1 GiB of HBM per device.

v0:
```python
import jax
import jax.numpy as jnp
from jax import lax
from jax.sharding import PartitionSpec as P

EPSILON = 1e-5
ROPE_BASE = 10000.0


def layer_norm(tok_rows, norm_params):
    rows_f32 = tok_rows.astype(jnp.float32)
    row_mean = jnp.mean(rows_f32, axis=-1, keepdims=True)
    centered = rows_f32 - row_mean
    row_var = jnp.mean(centered * centered, axis=-1, keepdims=True)
    normed = centered * lax.rsqrt(row_var + EPSILON)
    return (normed * norm_params[0].astype(jnp.float32) + norm_params[1].astype(jnp.float32)).astype(jnp.bfloat16)


def rotary_tables(pos_rows, head_dim):
    half_dim = head_dim // 2
    inv_freq = ROPE_BASE ** (-jnp.arange(half_dim, dtype=jnp.float32) * 2.0 / head_dim)
    angles = pos_rows.astype(jnp.float32)[..., None] * inv_freq
    return jnp.cos(angles), jnp.sin(angles)


def apply_rotary(vec, cos_table, sin_table):
    half_dim = vec.shape[-1] // 2
    vec_f32 = vec.astype(jnp.float32)
    first_half = vec_f32[..., :half_dim]
    second_half = vec_f32[..., half_dim:]
    return jnp.concatenate([first_half * cos_table - second_half * sin_table, second_half * cos_table + first_half * sin_table], axis=-1).astype(jnp.bfloat16)


def attention(qkv_rows, prompt_len, cos_table, sin_table, kv_heads, head_dim):
    num_prompts, seq_len = qkv_rows.shape[0], qkv_rows.shape[1]
    grouped = qkv_rows.reshape(num_prompts, seq_len, kv_heads, -1, head_dim)
    q_per = grouped.shape[3] - 2
    query_rot = apply_rotary(grouped[:, :, :, :q_per, :], cos_table[:, :, None, None, :], sin_table[:, :, None, None, :])
    key_rot = apply_rotary(grouped[:, :, :, q_per, :], cos_table[:, :, None, :], sin_table[:, :, None, :])
    value_rows = grouped[:, :, :, q_per + 1, :]
    scores = jnp.einsum('bqgph,bkgh->bgpqk', query_rot, key_rot, preferred_element_type=jnp.float32) * head_dim ** -0.5
    q_index = jnp.arange(seq_len)[:, None]
    k_index = jnp.arange(seq_len)[None, :]
    allowed = (k_index <= q_index)[None] & (k_index[None] < prompt_len[:, None, None])
    scores = jnp.where(allowed[:, None, None], scores, -1e30)
    prob_bf16 = jax.nn.softmax(scores, axis=-1).astype(jnp.bfloat16)
    context = jnp.einsum('bgpqk,bkgh->bqgph', prob_bf16, value_rows, preferred_element_type=jnp.float32).astype(jnp.bfloat16)
    return context, key_rot, value_rows


def decoder_layer(x, prompt_len, cos_table, sin_table, ln_a, ln_m, w_qkv, w_out, w_up, w_down):
    num_heads, head_dim = w_out.shape[0], w_out.shape[1]
    kv_heads = (w_qkv.shape[1] // head_dim - num_heads) // 2
    h_attn = layer_norm(x, ln_a)
    h_mlp = layer_norm(x, ln_m)
    qkv_rows = jnp.einsum('bsd,df->bsf', h_attn, w_qkv, preferred_element_type=jnp.float32).astype(jnp.bfloat16)
    context, key_rot, value_rows = attention(qkv_rows, prompt_len, cos_table, sin_table, kv_heads, head_dim)
    w_out_grouped = w_out.reshape(kv_heads, num_heads // kv_heads, head_dim, -1)
    attn_out = jnp.einsum('bsgph,gphd->bsd', context, w_out_grouped, preferred_element_type=jnp.float32)
    hidden = jax.nn.gelu(jnp.einsum('bsd,df->bsf', h_mlp, w_up, preferred_element_type=jnp.float32), approximate=False).astype(jnp.bfloat16)
    mlp_out = jnp.einsum('bsf,fd->bsd', hidden, w_down, preferred_element_type=jnp.float32)
    new_rows = (x.astype(jnp.float32) + attn_out + mlp_out).astype(jnp.bfloat16)
    return new_rows, key_rot, value_rows


def solution(mesh):
    batch_spec = P(('dp', 'wg'))
    col_spec = P(None, None, 'wg')
    out_spec = P(None, None, None, 'wg')
    cache_spec = P(None, ('dp', 'wg'))

    def local_program(x, positions, prompt_len, ln_attn, ln_mlp, w_qkv, w_out, w_up, w_down):
        cos_table, sin_table = rotary_tables(positions, w_out.shape[2])
        hidden_rows = x
        key_list = []
        value_list = []
        for layer_idx in range(w_qkv.shape[0]):
            ln_a = lax.all_gather(ln_attn[layer_idx], 'wg', axis=1, tiled=True)
            ln_m = lax.all_gather(ln_mlp[layer_idx], 'wg', axis=1, tiled=True)
            qkv_full = lax.all_gather(w_qkv[layer_idx], 'wg', axis=1, tiled=True)
            out_full = lax.all_gather(w_out[layer_idx], 'wg', axis=2, tiled=True)
            up_full = lax.all_gather(w_up[layer_idx], 'wg', axis=1, tiled=True)
            down_full = lax.all_gather(w_down[layer_idx], 'wg', axis=1, tiled=True)
            hidden_rows, key_rot, value_rows = decoder_layer(hidden_rows, prompt_len, cos_table[None], sin_table[None], ln_a, ln_m, qkv_full, out_full, up_full, down_full)
            key_list.append(key_rot)
            value_list.append(value_rows)
        return hidden_rows, jnp.stack(key_list), jnp.stack(value_list)

    return jax.shard_map(local_program, mesh=mesh, in_specs=(batch_spec, P('dp'), batch_spec, col_spec, col_spec, col_spec, out_spec, col_spec, col_spec), out_specs=(batch_spec, cache_spec, cache_spec), check_vma=False)
```

profile of v0, /device:TPU:0, one launch (start us, length us, event | category | flops | bytes accessed | tf_op | source)
XLA Modules:
  0.0 1595.3 jit_solution(1399811014871774573)
XLA Ops:
  7.2 0.0 all-gather.23.cloned.1.call-start
  7.2 3.8 fusion.356
  11.0 4.5 copy.69
  15.5 0.0 all-gather.31.cloned.1.call-start
  15.6 3.0 copy.75
  18.6 0.0 all-gather.21.cloned.1.call-start
  18.6 8.3 fusion.355
  27.0 0.0 all-gather.25.cloned.1.call-start
  27.0 10.4 fusion.353
  37.5 0.0 all-gather.27.cloned.1.call-start
  37.6 10.4 fusion.354
  48.0 0.0 all-gather.29.cloned.1.call-start
  48.0 0.5 all-gather.29.cloned.1.call-update
  48.6 0.7 all-gather.33.cloned.1.call-update
  49.4 0.7 all-gather.35.cloned.1.call-update
  50.1 0.2 copy.65
  50.9 0.2 copy.70
  51.1 0.2 copy.71
  51.3 0.2 copy.76
  51.4 27.0 %all-gather = bf16[1,2,2560]{1,0,2:T(2,128)(2,1)S(1)} all-gather(bf16[1,2,320]{1,0,2:T(2,128)(2,1)S(1)} %copy.65), channel_id=2, replica_groups=mesh['dp'=1,'wg'=8] {'wg'}, dimensions={2}, use_global_device_ids=true | all-gather | bytes 11520 | tf_op jit(solution)/shard_map/all_gather | solution.py:78
  78.4 24.6 %all-gather.3 = bf16[1,2,2560]{1,0,2:T(2,128)(2,1)S(1)} all-gather(bf16[1,2,320]{1,0,2:T(2,128)(2,1)S(1)} %copy.70), channel_id=5, replica_groups=mesh['dp'=1,'wg'=8] {'wg'}, dimensions={2}, use_global_device_ids=true | all-gather | bytes 11520 | tf_op jit(solution)/shard_map/all_gather | solution.py:79
  103.0 26.6 %all-gather.6 = bf16[1,2,2560]{1,0,2:T(2,128)(2,1)S(1)} all-gather(bf16[1,2,320]{1,0,2:T(2,128)(2,1)S(1)} %copy.71), channel_id=8, replica_groups=mesh['dp'=1,'wg'=8] {'wg'}, dimensions={2}, use_global_device_ids=true | all-gather | bytes 11520 | tf_op jit(solution)/shard_map/all_gather | solution.py:78
  129.7 19.0 %all-gather.9 = bf16[1,2,2560]{1,0,2:T(2,128)(2,1)S(1)} all-gather(bf16[1,2,320]{1,0,2:T(2,128)(2,1)S(1)} %copy.76), channel_id=11, replica_groups=mesh['dp'=1,'wg'=8] {'wg'}, dimensions={2}, use_global_device_ids=true | all-gather | bytes 11520 | tf_op jit(solution)/shard_map/all_gather | solution.py:79
  148.7 0.3 convert_reduce_fusion.1
  148.9 0.5 fusion.193
  149.5 0.1 fusion.282
  149.6 0.2 multiply_cosine_fusion
  149.8 41.3 %fusion.231 = (f32[2560]{0:T(1024)S(1)}, f32[2560]{0:T(1024)S(1)}) fusion(bf16[1,2,2560]{1,0,2:T(2,128)(2,1)S(1)} %all-gather), kind=kLoop, calls=%fused_computation.197 | loop fusion | flops 5120 | bytes 30720 | tf_op jit(solution)/shard_map/convert_element_type | solution.py:16
  191.1 41.5 %fusion.227 = (f32[2560]{0:T(1024)S(1)}, f32[2560]{0:T(1024)S(1)}) fusion(bf16[1,2,2560]{1,0,2:T(2,128)(2,1)S(1)} %all-gather.3), kind=kLoop, calls=%fused_computation.189 | loop fusion | flops 5120 | bytes 30720 | tf_op jit(solution)/shard_map/convert_element_type | solution.py:16
  232.6 42.3 %fusion.225 = (f32[2560]{0:T(1024)}, f32[2560]{0:T(1024)}) fusion(bf16[1,2,2560]{1,0,2:T(2,128)(2,1)S(1)} %all-gather.6), kind=kLoop, calls=%fused_computation.185 | loop fusion | flops 5120 | bytes 30720 | tf_op jit(solution)/shard_map/convert_element_type | solution.py:16
  274.9 42.1 %fusion.221 = (f32[2560]{0:T(1024)}, f32[2560]{0:T(1024)}) fusion(bf16[1,2,2560]{1,0,2:T(2,128)(2,1)S(1)} %all-gather.9), kind=kLoop, calls=%fused_computation.177 | loop fusion | flops 5120 | bytes 30720 | tf_op jit(solution)/shard_map/convert_element_type | solution.py:16
  317.0 26.1 %copy.52 = bf16[1,32,80,2560]{3,2,1,0:T(8,128)(2,1)} copy(bf16[1,32,80,2560]{2,1,0,3:T(8,128)(2,1)} %all-gather.23.cloned.1.call-done) | data formatting | bytes 26214400 | tf_op jit(solution)/shard_map/all_gather | solution.py:81
  343.1 26.0 %copy.61 = bf16[1,32,80,2560]{3,2,1,0:T(8,128)(2,1)} copy(bf16[1,32,80,2560]{2,1,0,3:T(8,128)(2,1)} %all-gather.31.cloned.1.call-done) | data formatting | bytes 26214400 | tf_op jit(solution)/shard_map/all_gather | solution.py:81
  369.1 64.4 %all-gather.21.cloned.1.call-done = bf16[1,2560,7680]{1,2,0:T(8,128)(2,1)} async-done(((bf16[1,2560,960]{1,2,0:T(8,128)(2,1)}), bf16[1,2560,7680]{1,2,0:T(8,128)(2,1)}) %all-gather.21.cloned.1.call-update) | async-done | bytes 39321616 | tf_op jit(solution)/shard_map/all_gather | solution.py:80
  433.5 18.9 %fusion.36 = bf16[256,7680]{1,0:T(8,128)(2,1)} fusion(bf16[1,2560,7680]{1,2,0:T(8,128)(2,1)} %all-gather.21.cloned.1.call-done, bf16[1,256,2560]{2,1,0:T(8,128)(2,1)S(1)} %copy-done.3, f32[2560]{0:T(1024)S(1)} %get-tuple-element.10, f32[2560]{0:T(1024)S(1)} %get-tuple-element.9, f32[256]{0:T(256)S(1)} %add_rsqrt_fusion.1, f32[256]{0:T(256)S(1)} %broadcast_multiply_fusion.1), kind=kOutput, calls=%fused_computation.54 | convolution fusion | flops 10072227840 | bytes 44587008 | tf_op jit(solution)/shard_map/bsd,df->bsf/dot_general | solution.py:56
  452.4 6.3 copy.46
  458.7 3.9 slice_bitcast_fusion.5
  462.6 0.4 subtract_convert_fusion.3
  463.1 0.4 fusion.278
  463.5 1.6 fusion.44
  465.1 3.2 copy-done.1
  468.2 1.9 fusion.42
  470.1 14.7 fusion.159
  484.8 185.1 %all-gather.25.cloned.1.call-done = bf16[1,2560,10240]{2,1,0:T(8,128)(2,1)} async-done(((bf16[1,2560,1280]{2,1,0:T(8,128)(2,1)}), bf16[1,2560,10240]{2,1,0:T(8,128)(2,1)}) %all-gather.25.cloned.1.call-update) | async-done | bytes 52428816 | tf_op jit(solution)/shard_map/all_gather | solution.py:82
  669.9 42.0 %fusion.168.clone.4 = bf16[256,10240]{1,0:T(8,128)(2,1)} fusion(bf16[1,2560,10240]{2,1,0:T(8,128)(2,1)} %all-gather.25.cloned.1.call-done, bf16[1,256,2560]{2,1,0:T(8,128)(2,1)S(1)} %copy-done.3, f32[2560]{0:T(1024)S(1)} %get-tuple-element.8, f32[2560]{0:T(1024)S(1)} %get-tuple-element.7, ...), kind=kOutput, calls=%fused_computation.20.clone.clone.clone.clone.clone.clone.clone.clone.clone.clone.1 | convolution fusion | flops 13596098560 | bytes 59004928 | tf_op jit(solution)/shard_map/bsd,df->bsf/dot_general | solution.py:60
  712.0 195.1 %all-gather.27.cloned.1.call-done = bf16[1,10240,2560]{1,2,0:T(8,128)(2,1)} async-done(((bf16[1,10240,320]{1,2,0:T(8,128)(2,1)}), bf16[1,10240,2560]{1,2,0:T(8,128)(2,1)}) %all-gather.27.cloned.1.call-update) | async-done | bytes 52428816 | tf_op jit(solution)/shard_map/all_gather | solution.py:83
  907.0 24.4 %convert_reduce_fusion = (f32[256]{0:T(256)S(1)}, bf16[1,256,2560]{2,1,0:T(8,128)(2,1)S(1)}) fusion(f32[1,256,2560]{2,1,0:T(8,128)} %fusion.159, bf16[1,10240,2560]{1,2,0:T(8,128)(2,1)} %all-gather.27.cloned.1.call-done, bf16[256,10240]{1,0:T(8,128)(2,1)} %fusion.168.clone.4), kind=kOutput, calls=%fused_computation.141 | convolution fusion | flops 13424394240 | bytes 61604864 | tf_op jit(solution)/shard_map/bsf,fd->bsd/dot_general | solution.py:61
  931.5 0.5 fusion.192
  932.0 157.4 %all-gather.29.cloned.1.call-done = bf16[1,2560,7680]{1,2,0:T(8,128)(2,1)} async-done(((bf16[1,2560,960]{1,2,0:T(8,128)(2,1)}), bf16[1,2560,7680]{1,2,0:T(8,128)(2,1)}) %all-gather.29.cloned.1.call-update) | async-done | bytes 39321616 | tf_op jit(solution)/shard_map/all_gather | solution.py:80
  1089.3 18.9 %fusion.39 = bf16[256,7680]{1,0:T(8,128)(2,1)} fusion(bf16[1,2560,7680]{1,2,0:T(8,128)(2,1)} %all-gather.29.cloned.1.call-done, bf16[1,256,2560]{2,1,0:T(8,128)(2,1)S(1)} %get-tuple-element.42, f32[2560]{0:T(1024)S(1)} %copy-done.17, f32[2560]{0:T(1024)S(1)} %copy-done.16, f32[256]{0:T(256)S(1)} %add_rsqrt_fusion, f32[256]{0:T(256)S(1)} %broadcast_multiply_fusion), kind=kOutput, calls=%fused_computation.55 | convolution fusion | flops 10072227840 | bytes 44587008 | tf_op jit(solution)/shard_map/bsd,df->bsf/dot_general | solution.py:56
  1108.2 6.3 copy.55
  1114.5 3.0 slice_bitcast_fusion.4
  1117.5 1.7 pad_maximum_fusion
  1119.2 0.4 subtract_convert_fusion.1
  1119.6 1.6 maximum_maximum_fusion
  1121.2 0.4 fusion.280
  1121.6 1.6 fusion.45
  1123.2 3.2 copy-done
  1126.4 1.9 fusion.43
  1128.3 14.8 fusion.156
  1143.1 182.8 %all-gather.33.cloned.1.call-done = bf16[1,2560,10240]{2,1,0:T(8,128)(2,1)} async-done(((bf16[1,2560,1280]{2,1,0:T(8,128)(2,1)}), bf16[1,2560,10240]{2,1,0:T(8,128)(2,1)}) %all-gather.33.cloned.1.call-update) | async-done | bytes 52428816 | tf_op jit(solution)/shard_map/all_gather | solution.py:82
  1325.9 41.7 %fusion.379 = bf16[256,10240]{1,0:T(8,128)(2,1)} fusion(bf16[1,2560,10240]{2,1,0:T(8,128)(2,1)} %all-gather.33.cloned.1.call-done, bf16[1,256,2560]{2,1,0:T(8,128)(2,1)S(1)} %get-tuple-element.42, f32[2560]{0:T(1024)S(1)} %copy-done.15, f32[2560]{0:T(1024)S(1)} %copy-done.14, f32[256]{0:T(256)S(1)} %add_rsqrt_fusion, ...), kind=kOutput, calls=%fused_computation.23.clone.clone.clone.clone.clone.clone.clone.clone.1 | convolution fusion | flops 13596098560 | bytes 59004928 | tf_op jit(solution)/shard_map/bsd,df->bsf/dot_general | solution.py:60
  1367.6 195.5 %all-gather.35.cloned.1.call-done = bf16[1,10240,2560]{1,2,0:T(8,128)(2,1)} async-done(((bf16[1,10240,320]{1,2,0:T(8,128)(2,1)}), bf16[1,10240,2560]{1,2,0:T(8,128)(2,1)}) %all-gather.35.cloned.1.call-update) | async-done | bytes 52428816 | tf_op jit(solution)/shard_map/all_gather | solution.py:83
  1563.1 25.1 %fusion.169 = bf16[1,256,2560]{2,1,0:T(8,128)(2,1)} fusion(f32[1,256,2560]{2,1,0:T(8,128)} %fusion.156, bf16[1,10240,2560]{1,2,0:T(8,128)(2,1)} %all-gather.35.cloned.1.call-done, bf16[256,10240]{1,0:T(8,128)(2,1)} %fusion.379), kind=kOutput, calls=%fused_computation.145 | convolution fusion | flops 13423083520 | bytes 61603840 | tf_op jit(solution)/shard_map/bsf,fd->bsd/dot_general | solution.py:61
  (58 shorter events, 0.3 us)
Async XLA Ops:
  7.2 309.8 %all-gather.23.cloned.1.call-start = ((), (), s32[]{:S(2)}) async-start(), calls=%async_computation.1 | async-start | bytes 23592960 | tf_op jit(solution)/shard_map/all_gather | solution.py:81
  15.5 327.5 %all-gather.31.cloned.1.call-start = ((), (), s32[]{:S(2)}) async-start(), calls=%async_computation.5 | async-start | bytes 23592960 | tf_op jit(solution)/shard_map/all_gather | solution.py:81
  18.6 414.9 %all-gather.21.cloned.1.call-start = ((), (), s32[]{:S(2)}) async-start(), calls=%async_computation | async-start | bytes 44236800 | tf_op jit(solution)/shard_map/all_gather | solution.py:80
  27.0 642.9 %all-gather.25.cloned.1.call-start = ((), (), s32[]{:S(2)}) async-start(), calls=%async_computation.2 | async-start | bytes 58982400 | tf_op jit(solution)/shard_map/all_gather | solution.py:82
  37.5 869.5 %all-gather.27.cloned.1.call-start = ((), (), s32[]{:S(2)}) async-start(), calls=%async_computation.3 | async-start | bytes 58982400 | tf_op jit(solution)/shard_map/all_gather | solution.py:83
  48.0 1041.4 %all-gather.29.cloned.1.call-start = ((), (), s32[]{:S(2)}) async-start(), calls=%async_computation.4 | async-start | bytes 44236800 | tf_op jit(solution)/shard_map/all_gather | solution.py:80
  48.5 1277.3 %all-gather.33.cloned.1.call-start = ((), (), s32[]{:S(2)}) async-start(), calls=%async_computation.6 | async-start | bytes 58982400 | tf_op jit(solution)/shard_map/all_gather | solution.py:82
  48.6 1.5 copy-start.18
  48.6 1.6 copy-start.20
  48.6 2.3 copy-start.19
  49.3 1513.8 %all-gather.35.cloned.1.call-start = ((), (), s32[]{:S(2)}) async-start(), calls=%async_computation.7 | async-start | bytes 58982400 | tf_op jit(solution)/shard_map/all_gather | solution.py:83
  49.3 99.3 %copy-start.3 = (bf16[1,256,2560]{2,1,0:T(8,128)(2,1)S(1)}, bf16[1,256,2560]{2,1,0:T(8,128)(2,1)}, u32[]{:S(2)}) copy-start(bf16[1,256,2560]{2,1,0:T(8,128)(2,1)} %param.9) | copy-start | bytes 3932164
  149.6 320.5 %copy-start.12 = (pred[256,256]{0,1:T(8,128)(4,1)}, pred[256,256]{0,1:T(8,128)(4,1)S(1)}, u32[]{:S(2)}) copy-start(pred[256,256]{0,1:T(8,128)(4,1)S(1)} %fusion.282) | copy-start | bytes 196612
  149.8 313.2 %copy-start.8 = (f32[256,40]{0,1:T(8,128)}, f32[256,40]{0,1:T(8,128)S(1)}, u32[]{:S(2)}) copy-start(f32[256,40]{0,1:T(8,128)S(1)} %get-tuple-element.37) | copy-start | bytes 122884
  149.8 313.2 %copy-start.10 = (f32[256,40]{0,1:T(8,128)}, f32[256,40]{0,1:T(8,128)S(1)}, u32[]{:S(2)}) copy-start(f32[256,40]{0,1:T(8,128)S(1)} %get-tuple-element.38) | copy-start | bytes 122884
  463.0 2.0 copy-start.4
  463.0 2.0 copy-start.6
  465.1 3.2 copy-start.1
  712.0 377.4 %copy-start.16 = (f32[2560]{0:T(1024)S(1)}, f32[2560]{0:T(1024)}, u32[]{:S(2)}) copy-start(f32[2560]{0:T(1024)} %get-tuple-element.5) | copy-start | bytes 30724
  712.0 377.4 %copy-start.17 = (f32[2560]{0:T(1024)S(1)}, f32[2560]{0:T(1024)}, u32[]{:S(2)}) copy-start(f32[2560]{0:T(1024)} %get-tuple-element.6) | copy-start | bytes 30724
  1114.5 3.0 copy-start.2
  1114.5 4.8 copy-start.9
  1114.5 4.8 copy-start.11
  1117.5 2.2 copy-start.5
  1117.5 2.2 copy-start.7
  1119.2 2.4 copy-start.13
  1123.2 3.2 copy-start
  1128.3 197.6 %copy-start.14 = (f32[2560]{0:T(1024)S(1)}, f32[2560]{0:T(1024)}, u32[]{:S(2)}) copy-start(f32[2560]{0:T(1024)} %get-tuple-element.3) | copy-start | bytes 30724
  1128.3 197.6 %copy-start.15 = (f32[2560]{0:T(1024)S(1)}, f32[2560]{0:T(1024)}, u32[]{:S(2)}) copy-start(f32[2560]{0:T(1024)} %get-tuple-element.4) | copy-start | bytes 30724
Sparse Core Ops, SparseCore 0:
  15.7 130.9 all-gather.22
  149.1 101.9 all-gather.30
  252.9 180.5 all-gather.20
  435.2 234.6 all-gather.24
  671.6 235.3 all-gather.26
  908.7 180.5 all-gather.28
  1091.2 234.6 all-gather.32
  1327.7 235.3 all-gather.34
where the time goes:
time: 1600 us
  waiting for transfers between devices  982 us (61%)
  matrix products  204 us (13%)
  other arithmetic  184 us (12%)
  local copies, waits for them, and re-layouts  112 us (7%)
  blocking collectives  97.2 us (6%)
    all_gather x2, waiting for transfers between devices, local_program(): down_full = lax.all_gather(w_down[layer_idx], 'wg', axis=1, tiled=True)  391 us
    all_gather x2, waiting for transfers between devices, local_program(): up_full = lax.all_gather(w_up[layer_idx], 'wg', axis=1, tiled=True)  368 us
    all_gather x2, waiting for transfers between devices, local_program(): qkv_full = lax.all_gather(w_qkv[layer_idx], 'wg', axis=1, tiled=True)  222 us
    convert_element_type x4, other arithmetic, layer_norm(): norm_params[0].astype(jnp.float32)  167 us
    dot_general x2, matrix products, decoder_layer(): jnp.einsum('bsd,df->bsf', h_mlp, w_up, preferred_element_type=jnp.float32)  83.8 us
    all_gather x2, blocking collectives, local_program(): ln_a = lax.all_gather(ln_attn[layer_idx], 'wg', axis=1, tiled=True)  53.6 us
    all_gather x2, local copies, waits for them, and re-layouts, local_program(): out_full = lax.all_gather(w_out[layer_idx], 'wg', axis=2, tiled=True)  52.1 us
    dot_general x2, matrix products, decoder_layer(): jnp.einsum('bsf,fd->bsd', hidden, w_down, preferred_element_type=jnp.floa...  49.5 us
  transfers between devices with their start and end apart: 8, of which 6 were waited for; matrix products, arithmetic and copies ran while one was open for 29% of the time, Pallas kernels for 0%

commit v1 on v0

v1 whole, which is shorter than its diff:
```python
import jax
import jax.numpy as jnp
from jax import lax
from jax.experimental import pallas as pl
from jax.experimental.pallas import tpu as pltpu
from jax.sharding import PartitionSpec as P

EPSILON = 1e-5
ROPE_BASE = 10000.0
F32 = jnp.float32
BF16 = jnp.bfloat16
MESH = pl.DeviceIdType.MESH
NT = (((1,), (1,)), ((), ()))
TN = (((0,), (0,)), ((), ()))
TT = (((0,), (1,)), ((), ()))


def flip(v, s):
    if s & 1:
        v = v + 1 - 2 * (v % 2)
    if s & 2:
        v = v + 2 - 4 * ((v // 2) % 2)
    if s & 4:
        v = v + 4 - 8 * ((v // 4) % 2)
    return v


def make_kernel(cfg):
    n, layers, seq, d, heads, hd, hid = (cfg[k] for k in ('n', 'layers', 'seq', 'd', 'heads', 'hd', 'hid'))
    two = 2 * seq
    cc = heads * hd
    half_d = d // 2
    hs = seq // 2
    slot = 3 * hd
    half_hd = hd // 2
    tile = 256
    hid_tiles, out_tiles = hid // tile, half_d // tile
    ncols = d // n
    win = ncols + 64

    def kernel(x_ref, wq_ref, wu_ref, wd_ref, wo_ref, ln_ref, cos_ref, sin_ref,
               y_ref, kv_ref, xg_ref, w2_ref, hrec_ref, crec_ref,
               wq, wu, w2v, xbuf, abuf, mbuf, hbuf, hr, kvb, cbuf, p2, p31, p0, pd3, pd1, px, nbuf, lnrec, lnf,
               ssem, rsem, lsem):
        me = lax.axis_index('wg')
        yb = me // 4
        q = me % 4
        row = pl.multiple_of(seq * yb, seq)
        orow = pl.multiple_of(seq * (1 - yb), seq)
        ycol = pl.multiple_of(half_d * yb, half_d)
        ocol = pl.multiple_of(half_d * (1 - yb), half_d)
        counter = [0, 0]

        def take(k=1):
            counter[0] += k
            return counter[0] - k

        def rc(src, dst, s, idx=None):
            i = take() if idx is None else idx
            return pltpu.make_async_remote_copy(src_ref=src, dst_ref=dst, send_sem=ssem.at[i], recv_sem=rsem.at[i],
                                                device_id={'wg': flip(me, s)}, device_id_type=MESH)

        def lc(src, dst):
            counter[1] += 1
            return pltpu.make_async_copy(src, dst, lsem.at[counter[1] - 1])

        def start(*cs):
            for c in cs:
                c.start()
            return cs

        def waits(cs):
            for c in cs:
                c.wait_send()

        def recvs(cs):
            for c in cs:
                c.wait_recv()

        def waitl(cs):
            for c in cs:
                c.wait()

        barrier = pltpu.get_barrier_semaphore()
        for s in range(1, n):
            pl.semaphore_signal(barrier, inc=1, device_id={'wg': flip(me, s)}, device_id_type=MESH)
        pl.semaphore_wait(barrier, n - 1)

        sent = []
        lnc = [rc(ln_ref, lnrec.at[me], s) for s in range(1, n)]
        start(*lnc)
        lnl = start(lc(ln_ref, lnrec.at[me]))

        def load_first(l):
            return start(lc(wq_ref.at[l], wq), lc(wu_ref.at[l], wu))

        def gather0():
            xt, g = x_ref, xg_ref.at[0]
            y1 = rc(xt.at[pl.ds(0, hs)], g.at[0, pl.ds(row, hs)], 4)
            y2 = rc(xt.at[pl.ds(hs, hs)], g.at[0, pl.ds(row + hs, hs)], 4)
            x1 = rc(xt.at[pl.ds(hs, hs)], g.at[2, pl.ds(row + hs, hs)], 2)
            x2 = rc(xt.at[pl.ds(0, hs)], g.at[2, pl.ds(row, hs)], 2)
            c0 = rc(xt, g.at[1, pl.ds(row, seq)], 1)
            start(y1, x1, y2, x2, c0)
            y1.wait_recv()
            rx = rc(g.at[0, pl.ds(orow, hs)], g.at[2, pl.ds(orow, hs)], 2)
            rx.start()
            x1.wait_recv()
            ry = rc(g.at[2, pl.ds(row + hs, hs)], g.at[2, pl.ds(row + hs, hs)], 4)
            ry.start()
            y2.wait_recv()
            c1 = rc(g.at[0, pl.ds(orow, seq)], g.at[1, pl.ds(orow, seq)], 1)
            c1.start()
            sent.extend([y1, y2, x1, x2, c0, rx, ry, c1])

            def rest():
                x2.wait_recv()
                c2 = rc(g.at[2, pl.ds(row, seq)], g.at[3, pl.ds(row, seq)], 1)
                c2.start()
                recvs([rx, ry])
                c3 = rc(g.at[2, pl.ds(orow, seq)], g.at[3, pl.ds(orow, seq)], 1)
                c3.start()
                sent.extend([c2, c3])
                return [c2, c3]
            return rest, [c0, c1]

        def gather1(l):
            g = xg_ref.at[l]
            lo, hi = pl.ds(0, seq), pl.ds(seq, seq)
            yc, oc = pl.ds(ycol, half_d), pl.ds(ocol, half_d)
            y1 = rc(nbuf.at[lo], g.at[0, lo, yc], 4)
            y2 = rc(nbuf.at[hi], g.at[0, hi, yc], 4)
            x1 = rc(nbuf.at[hi], g.at[2, hi, yc], 2)
            x2 = rc(nbuf.at[lo], g.at[2, lo, yc], 2)
            start(y1, x1, y2, x2)
            own = start(lc(nbuf, g.at[0, :, yc]))
            y1.wait_recv()
            rx = rc(g.at[0, lo, oc], g.at[2, lo, oc], 2)
            rx.start()
            x1.wait_recv()
            ry = rc(g.at[2, hi, yc], g.at[2, hi, yc], 4)
            ry.start()
            y2.wait_recv()
            waitl(own)
            c1 = rc(g.at[0], g.at[1], 1)
            c1.start()
            sent.extend([y1, y2, x1, x2, rx, ry, c1])

            def rest():
                recvs([x2, rx, ry])
                c3 = rc(g.at[2], g.at[3], 1)
                c3.start()
                sent.append(c3)
                return [c3]
            return rest, [c1]

        def send_weights(l):
            rows = pl.ds(pl.multiple_of(cc * q, 64), cc)
            out = []
            for r in (2, 3, 1):
                t = flip(me, r)
                ty = flip(t, 4)
                out.append(rc(wd_ref.at[l, :, pl.ds(pl.multiple_of(hid * t, 128), hid)], w2_ref.at[l, rows, pl.ds(0, hid)], r))
                out.append(rc(wd_ref.at[l, :, pl.ds(pl.multiple_of(hid * ty, 128), hid)], w2_ref.at[l, rows, pl.ds(hid, hid)], r))
                out.append(rc(wo_ref.at[l, t % 4], w2_ref.at[l, rows, pl.ds(2 * hid, 2 * cc)], r))
            start(*out)
            sent.extend(out)
            return out

        def own_weights(l):
            rows = pl.ds(pl.multiple_of(cc * q, 64), cc)
            return start(
                lc(wd_ref.at[l, :, pl.ds(pl.multiple_of(hid * me, 128), hid)], w2v.at[rows, pl.ds(0, hid)]),
                lc(wd_ref.at[l, :, pl.ds(pl.multiple_of(hid * flip(me, 4), 128), hid)], w2v.at[rows, pl.ds(hid, hid)]),
                lc(wo_ref.at[l, q], w2v.at[rows, pl.ds(2 * hid, 2 * cc)]))

        def other_weights(l, inbound):
            recvs(inbound)
            cs = []
            for r in (1, 2, 3):
                rows = pl.ds(pl.multiple_of(cc * flip(q, r), 64), cc)
                cs.append(lc(w2_ref.at[l, rows], w2v.at[rows]))
            return start(*cs)

        def load_x(l, r):
            if l == 0 and r == 0:
                return start(lc(x_ref, xbuf.at[pl.ds(row, seq)]), lc(xg_ref.at[0, 0, pl.ds(orow, seq)], xbuf.at[pl.ds(orow, seq)]))
            return start(lc(xg_ref.at[l, r], xbuf))

        def norm(l):
            @pl.loop(0, two // 16)
            def _(i):
                rs = pl.ds(pl.multiple_of(i * 16, 16), 16)
                v = xbuf[rs, :].astype(F32)
                cen = v - jnp.mean(v, axis=-1, keepdims=True)
                var = jnp.mean(cen * cen, axis=-1, keepdims=True)
                nrm = cen * lax.rsqrt(var + EPSILON)
                k = 4 * l
                abuf[rs, :] = (nrm * lnf[k:k + 1, :] + lnf[k + 1:k + 2, :]).astype(BF16)
                mbuf[rs, :] = (nrm * lnf[k + 2:k + 3, :] + lnf[k + 3:k + 4, :]).astype(BF16)

        def h_copy(l, r, t, base):
            cs = pl.ds(pl.multiple_of(t * tile, tile), tile)
            return rc(hbuf.at[r, :, cs], hrec_ref.at[l, r, :, cs], 4, base + t)

        def up(l, r, base):
            @pl.loop(0, hid_tiles)
            def _(t):
                cs = pl.ds(pl.multiple_of(t * tile, tile), tile)
                u = jnp.dot(mbuf[...], wu[:, cs], preferred_element_type=F32)
                hbuf[r, :, cs] = (0.5 * u * (1.0 + lax.erf(u * (0.5 ** 0.5)))).astype(BF16)
                h_copy(l, r, t, base).start()

        def attend(l, r):
            kidx = lax.broadcasted_iota(jnp.int32, (seq, seq), 0)
            qidx = lax.broadcasted_iota(jnp.int32, (seq, seq), 1)
            causal = kidx <= qidx
            kf = kidx.astype(F32)

            @pl.loop(0, heads)
            def _(h):
                t = lax.dot_general(wq[pl.ds(pl.multiple_of(h * slot, 16), slot), :], abuf[...], NT, preferred_element_type=F32)
                t = t.astype(BF16).astype(F32)
                cs, sn = cos_ref[...], sin_ref[...]

                def turn(v):
                    a, b = v[:half_hd], v[half_hd:]
                    return jnp.concatenate([a * cs - b * sn, b * cs + a * sn], axis=0).astype(BF16)
                qr, kr, vr = turn(t[:hd]), turn(t[hd:2 * hd]), t[2 * hd:].astype(BF16)
                hrow = pl.ds(pl.multiple_of(h * hd, 16), hd)
                kvb[r, 0, hrow, :] = kr
                kvb[r, 1, hrow, :] = vr
                crow = pl.ds(pl.multiple_of(cc * yb + h * hd, 16), hd)
                for j in range(2):
                    ps = slice(j * seq, (j + 1) * seq)
                    s = lax.dot_general(kr[:, ps], qr[:, ps], TN, preferred_element_type=F32) * hd ** -0.5
                    plen = lnrec[flip(q, r) + 4 * j, 8:9, 0:seq].astype(F32)
                    s = jnp.where(causal & (kf < plen), s, -1e30)
                    e = jnp.exp(s - jnp.max(s, axis=0, keepdims=True))
                    p = (e / jnp.sum(e, axis=0, keepdims=True)).astype(BF16)
                    cbuf[r, crow, ps] = jnp.dot(vr[:, ps], p, preferred_element_type=F32).astype(BF16)

        def first(l, r, prev):
            xs = load_x(l, r)
            if prev:
                waits(prev)
            waitl(xs)
            norm(l)
            base = take(hid_tiles)
            up(l, r, base)
            attend(l, r)
            crows = pl.ds(pl.multiple_of(cc * yb, 64), cc)
            c = rc(cbuf.at[r, crows], crec_ref.at[l, r], 4)
            c.start()
            hcs = [h_copy(l, r, t, base) for t in range(hid_tiles)]
            return hcs, c

        def kv_send(l, r, ys):
            j = yb if ys == 0 else 1 - yb
            src = kvb.at[r, :, :, pl.ds(pl.multiple_of(seq * j, seq), seq)]
            dst = kv_ref.at[l, :, pl.ds(pl.multiple_of(cc * me, 64), cc), :]
            s = 4 * ys + r
            c = lc(src, dst) if s == 0 else rc(src, dst, s)
            c.start()
            return c

        def second(l, r, hcs, c, dst, send_to, wait_before):
            recvs(hcs)
            c.wait_recv()
            orows = pl.ds(pl.multiple_of(cc * (1 - yb), 64), cc)
            cs = start(lc(hrec_ref.at[l, r], hr), lc(crec_ref.at[l, r], cbuf.at[r, orows]))
            waitl(cs)
            if wait_before:
                waits(wait_before)
            base = take(out_tiles) if send_to is not None else None

            def p_copy(t):
                ts = pl.ds(pl.multiple_of(t * tile, tile), tile)
                return rc(dst.at[:, ts], send_to.at[:, ts], 1, base + t)

            @pl.loop(0, out_tiles)
            def _(t):
                ts = pl.ds(pl.multiple_of(t * tile, tile), tile)
                acc = lax.dot_general(hbuf[r], w2v[ts, 0:hid], NT, preferred_element_type=F32)
                acc = acc + lax.dot_general(hr[...], w2v[ts, hid:2 * hid], NT, preferred_element_type=F32)
                acc = acc + lax.dot_general(cbuf[r], w2v[ts, 2 * hid:], TT, preferred_element_type=F32)
                dst[:, ts] = acc
                if send_to is not None:
                    p_copy(t).start()
            return [p_copy(t) for t in range(out_tiles)] if send_to is not None else []

        rest, near = gather0()
        lw = load_first(0)
        res0 = start(lc(x_ref.at[:, pl.ds(ycol, half_d)], nbuf.at[pl.ds(row, seq)]),
                     lc(xg_ref.at[0, 0, pl.ds(orow, seq), pl.ds(ycol, half_d)], nbuf.at[pl.ds(orow, seq)]))
        recvs(lnc)
        waitl(lnl)
        lnf[...] = jnp.zeros_like(lnf)
        for e in range(n):
            lo = ncols * e - 64 * (e % 2)
            lnf[:, lo:lo + win] += lnrec[e].astype(F32)
        wait_prev = {r: [] for r in range(4)}
        p_prev = {'p2': [], 'p31': []}
        kv_local = []
        for l in range(layers):
            inbound = send_weights(l)
            w_own = own_weights(l)
            waitl(lw)
            hc, xc = {}, {}
            hc[0], xc[0] = first(l, 0, wait_prev[0])
            far = rest()
            hc[2], xc[2] = first(l, 2, wait_prev[2])
            recvs(far)
            hc[3], xc[3] = first(l, 3, wait_prev[3])
            recvs(near)
            hc[1], xc[1] = first(l, 1, wait_prev[1])
            kvs = {r: [] for r in range(4)}
            for r in range(4):
                kvs[r].append(kv_send(l, r, 1))
            kvs[1].append(kv_send(l, 1, 0))
            if l + 1 < layers:
                lw = load_first(l + 1)
            w_in = other_weights(l, inbound)
            waitl(w_own)
            waitl(w_in)
            second(l, 2, hc[2], xc[2], p2, None, p_prev['p2'])
            c3 = second(l, 3, hc[3], xc[3], p31, pd3, p_prev['p31'])
            xbase = take(out_tiles)

            def x_copy(t):
                ts = pl.ds(t * tile, tile)
                return rc(p2.at[:, ts], px.at[:, ts], 2, xbase + t)
            for t in range(out_tiles):
                ts = slice(t * tile, (t + 1) * tile)
                c3[t].wait_recv()
                p2[:, ts] += pd3[:, ts]
                x_copy(t).start()
            xcs = [x_copy(t) for t in range(out_tiles)]
            kvs[2].append(kv_send(l, 2, 0))
            kvs[3].append(kv_send(l, 3, 0))
            loc = kv_send(l, 0, 0)
            c1 = second(l, 1, hc[1], xc[1], p31, pd1, c3)
            second(l, 0, hc[0], xc[0], p0, None, [])
            if l == 0:
                waitl(res0)
            else:
                waits(sent)
                sent.clear()
            for t in range(out_tiles):
                ts = slice(t * tile, (t + 1) * tile)
                c1[t].wait_recv()
                xcs[t].wait_recv()
                total = p0[:, ts] + pd1[:, ts] + px[:, ts]
                nbuf[:, ts] = (nbuf[:, ts].astype(F32) + total).astype(BF16)
            loc.wait()
            if l + 1 < layers:
                waits(sent)
                sent.clear()
                rest, near = gather1(l + 1)
                wait_prev = {r: hc[r] + [xc[r]] + kvs[r] for r in range(4)}
                p_prev = {'p2': xcs, 'p31': c1}
                recvs([c for r in range(4) for c in kvs[r]])
            else:
                fin = rc(nbuf.at[pl.ds(orow, seq)], y_ref.at[:, pl.ds(ycol, half_d)], 4)
                fin.start()
                loc = start(lc(nbuf.at[pl.ds(row, seq)], y_ref.at[:, pl.ds(ycol, half_d)]))
                waits(xcs + c1 + [c for r in range(4) for c in hc[r] + [xc[r]] + kvs[r]])
                recvs([c for r in range(4) for c in kvs[r]])
                fin.wait()
                waitl(loc)
        waits(lnc)
        assert counter[0] <= cfg['n_remote'] and counter[1] <= cfg['n_local'], counter
    return kernel


def solution(mesh):
    n = mesh.shape['wg']
    batch_spec = P(('dp', 'wg'))
    col_spec = P(None, None, 'wg')
    out_spec = P(None, None, None, 'wg')
    cache_spec = P(None, ('dp', 'wg'))

    def local_program(x, positions, prompt_len, ln_attn, ln_mlp, w_qkv, w_out, w_up, w_down):
        layers, d, _ = w_qkv.shape
        n_heads, hd = w_out.shape[1], w_out.shape[2]
        heads = n_heads // n
        seq, hid, cc = x.shape[1], w_up.shape[2], heads * hd
        two, half_d = 2 * seq, d // 2
        me = lax.axis_index('wg')
        cfg = dict(n=n, layers=layers, seq=seq, d=d, heads=heads, hd=hd, hid=hid, n_remote=192, n_local=96)
        half_hd = hd // 2
        inv_freq = ROPE_BASE ** (-jnp.arange(half_hd, dtype=F32) * 2.0 / hd)
        angles = positions.astype(F32)[None, :] * inv_freq[:, None]
        cos_t, sin_t = (jnp.tile(f(angles), (1, 2)) for f in (jnp.cos, jnp.sin))
        ln = jnp.concatenate([ln_attn, ln_mlp], axis=1).reshape(4 * layers, -1)
        wide = jnp.where(me % 2 == 1, jnp.pad(ln, ((0, 0), (64, 0))), jnp.pad(ln, ((0, 0), (0, 64))))
        win = wide.shape[1]
        lens = jnp.broadcast_to(prompt_len.astype(BF16)[:, None], (1, win))
        ln_piece = jnp.concatenate([wide, lens, jnp.zeros((16 - 4 * layers - 1, win), BF16)], axis=0)
        wq_t = w_qkv.transpose(0, 2, 1)
        wd_t = w_down.transpose(0, 2, 1)
        wo_t = w_out.reshape(layers, 2, 4, cc, cc).transpose(0, 2, 4, 1, 3).reshape(layers, 4, cc, 2 * cc)

        hbm = pl.BlockSpec(memory_space=pltpu.MemorySpace.HBM)
        vmem = pl.BlockSpec(memory_space=pltpu.MemorySpace.VMEM)
        sds = jax.ShapeDtypeStruct
        outs = pl.pallas_call(
            make_kernel(cfg),
            out_shape=[
                sds((seq, d), BF16), sds((layers, 2, d, seq), BF16), sds((layers, 4, two, d), BF16),
                sds((layers, half_d, 2 * hid + 2 * cc), BF16), sds((layers, 4, two, hid), BF16), sds((layers, 4, cc, two), BF16)],
            in_specs=[hbm] * 5 + [hbm, vmem, vmem],
            out_specs=[hbm] * 6,
            scratch_shapes=[
                pltpu.VMEM((3 * cc, d), BF16), pltpu.VMEM((d, hid), BF16), pltpu.VMEM((half_d, 2 * hid + 2 * cc), BF16),
                pltpu.VMEM((two, d), BF16), pltpu.VMEM((two, d), BF16), pltpu.VMEM((two, d), BF16),
                pltpu.VMEM((4, two, hid), BF16), pltpu.VMEM((two, hid), BF16),
                pltpu.VMEM((4, 2, cc, two), BF16), pltpu.VMEM((4, 2 * cc, two), BF16),
                pltpu.VMEM((two, half_d), F32), pltpu.VMEM((two, half_d), F32), pltpu.VMEM((two, half_d), F32),
                pltpu.VMEM((two, half_d), F32), pltpu.VMEM((two, half_d), F32), pltpu.VMEM((two, half_d), F32),
                pltpu.VMEM((two, half_d), BF16), pltpu.VMEM((n, 16, win), BF16), pltpu.VMEM((16, d), F32),
                pltpu.SemaphoreType.DMA((cfg['n_remote'],)), pltpu.SemaphoreType.DMA((cfg['n_remote'],)),
                pltpu.SemaphoreType.DMA((cfg['n_local'],))],
            compiler_params=pltpu.CompilerParams(collective_id=0, has_side_effects=True, vmem_limit_bytes=67043328),
        )(x[0], wq_t, w_up, wd_t, wo_t, ln_piece, cos_t, sin_t)
        y, kv = outs[0], outs[1]
        caches = [kv[:, i].reshape(layers, 1, n_heads, hd, seq).transpose(0, 1, 4, 2, 3) for i in range(2)]
        return y[None], caches[0], caches[1]

    return jax.shard_map(local_program, mesh=mesh, in_specs=(batch_spec, P('dp'), batch_spec, col_spec, col_spec, col_spec, out_spec, col_spec, col_spec), out_specs=(batch_spec, cache_spec, cache_spec), check_vma=False)
```

time: 1600 us -> 515 us (0.32)
  waiting for transfers between devices: 982 us -> 0 us
  Pallas kernels: 0 us -> 481 us
  matrix products: 204 us -> 0 us
  other arithmetic: 184 us -> 2.38 us
  blocking collectives: 97.2 us -> 0 us
  local copies, waits for them, and re-layouts: 112 us -> 28.9 us
    all_gather x8 -> x0, waiting for transfers between devices: 980 us -> none  [the longest x2 391 us: local_program(): down_full = lax.all_gather(w_down[layer_idx], 'wg', axis=1, tiled=True)]
    pallas_call x0 -> x1, Pallas kernels: none -> 481 us  [local_program(): pl.pallas_call(make_kernel(cfg), out_shape=[sds((seq, d), BF16), sds((lay...]
    dot_general x10 -> x0, matrix products: 204 us -> none  [the longest x2 83.8 us: decoder_layer(): jnp.einsum('bsd,df->bsf', h_mlp, w_up, preferred_element_type=jnp.float32)]
    convert_element_type x5 -> x1, other arithmetic: 167 us -> 0.69 us  [local_program(): angles = positions.astype(F32)[None, :] * inv_freq[:, None]]
    all_gather x4 -> x0, blocking collectives: 97.2 us -> none  [the longest x2 53.6 us: local_program(): ln_a = lax.all_gather(ln_attn[layer_idx], 'wg', axis=1, tiled=True)]
    all_gather x2 -> x0, local copies, waits for them, and re-layouts: 52.1 us -> none  [local_program(): out_full = lax.all_gather(w_out[layer_idx], 'wg', axis=2, tiled=True)]
    slice x6 -> x1, local copies, waits for them, and re-layouts: 33 us -> 5.33 us  [local_program(): kv[:, i].reshape(layers, 1, n_heads, hd, seq).transpose(0, 1, 4, 2, 3)]
    reshape x0 -> x3, local copies, waits for them, and re-layouts: none -> 21 us  [the longest x2 21 us: local_program(): w_out.reshape(layers, 2, 4, cc, cc).transpose(0, 2, 4, 1, 3)]
  transfers between devices with their start and end apart: 8 -> 0, of which waited for: 6 -> 0; matrix products, arithmetic and copies ran while one was open for 29% -> 0% of each run, Pallas kernels for 0% -> 0%
where the time goes in v1:
time: 515 us; the launch traced here: 513 us
  Pallas kernels  481 us (93%)
  local copies, waits for them, and re-layouts  28.9 us (6%)
    pallas_call x1, Pallas kernels, local_program(): pl.pallas_call(make_kernel(cfg), out_shape=[sds((seq, d), BF16), sds((lay...  481 us
    reshape x2, local copies, waits for them, and re-layouts, local_program(): w_out.reshape(layers, 2, 4, cc, cc).transpose(0, 2, 4, 1, 3)  21 us

profile of v1, /device:TPU:0, one launch (start us, length us, event | category | flops | bytes accessed | tf_op | source)
XLA Modules:
  0.0 513.4 jit_solution(8442936812245090466)
XLA Ops:
  1.3 0.1 pad.11.clone
  1.4 0.1 pad.12.clone
  1.5 0.7 convert_element_type.11
  2.1 0.7 pad_maximum_fusion
  2.9 0.1 pad_select_fusion
  3.0 0.7 maximum_maximum_fusion.ln_ref
  3.6 0.2 multiply_sine_fusion
  3.9 0.6 copy.16
  4.6 0.6 copy.15
  5.2 12.2 %copy.12 = bf16[2,2,4,320,320]{3,1,4,2,0:T(2,128)(2,1)} copy(bf16[2,2,4,320,320]{4,3,2,1,0:T(8,128)(2,1)} %bitcast.24) | data formatting | bytes 6553600 | tf_op jit(solution)/shard_map/reshape | solution.py:402
  17.4 8.8 %reshape.82.wo_ref = bf16[2,4,320,640]{3,2,1,0:T(8,128)(2,1)} reshape(bf16[2,4,320,2,320]{4,3,2,1,0:T(2,128)(2,1)} %bitcast.21) | data formatting | bytes 6553600 | tf_op jit(solution)/shard_map/reshape | solution.py:402
  26.2 480.8 %shard_map.112 = (bf16[256,2560]{1,0:T(8,128)(2,1)}, bf16[2,2,2560,256]{3,2,1,0:T(8,128)(2,1)}, bf16[2,4,512,2560]{3,2,1,0:T(8,128)(2,1)}, bf16[2,1280,3200]{2,1...) custom-call(bf16[256,2560]{1,0:T(8,128)(2,1)} %bitcast.27, ...), custom_call_target="tpu_custom_call" | custom-call | tf_op jit(solution)/shard_map/pallas_call | solution.py:407
  507.0 0.0 copy-start
  507.0 5.3 %fusion = (bf16[2,1,2560,256]{3,2,1,0:T(8,128)(2,1)}, bf16[2,1,2560,256]{3,2,1,0:T(8,128)(2,1)}) fusion(bf16[2,2,2560,256]{3,2,1,0:T(8,128)(2,1)} %get-tuple-element.6), kind=kLoop, calls=%fused_computation.6 | loop fusion | bytes 10485760 | tf_op jit(solution)/shard_map/slice | solution.py:427
  512.4 0.0 copy-done
  512.4 1.1 copy.19
  (5 shorter events, 0.1 us)
Async XLA Ops:
  507.0 5.3 %copy-start = (bf16[256,2560]{1,0:T(8,128)(2,1)S(1)}, bf16[256,2560]{1,0:T(8,128)(2,1)}, u32[]{:S(2)}) copy-start(bf16[256,2560]{1,0:T(8,128)(2,1)} %get-tuple-element.5) | copy-start | bytes 3932164

commit v2 on v1

--- a/solution.py
+++ b/solution.py
@@ -13,6 +13,7 @@
 NT = (((1,), (1,)), ((), ()))
 TN = (((0,), (0,)), ((), ()))
 TT = (((0,), (1,)), ((), ()))
+HELD = 2
 
 
 def flip(v, s):
@@ -40,7 +41,7 @@
 
     def kernel(x_ref, wq_ref, wu_ref, wd_ref, wo_ref, ln_ref, cos_ref, sin_ref,
                y_ref, kv_ref, xg_ref, w2_ref, hrec_ref, crec_ref,
-               wq, wu, w2v, xbuf, abuf, mbuf, hbuf, hr, kvb, cbuf, p2, p31, p0, pd3, pd1, px, nbuf, lnrec, lnf,
+               wq, wu, w2v, wob, wot, xbuf, abuf, mbuf, hbuf, hr, kvb, cbuf, p2, p31, p0, pd3, pd1, px, nbuf, lnrec, lnf,
                ssem, rsem, lsem):
         me = lax.axis_index('wg')
         yb = me // 4
@@ -91,6 +92,15 @@
         start(*lnc)
         lnl = start(lc(ln_ref, lnrec.at[me]))
 
+        def load_out(l):
+            return start(lc(wo_ref.at[l], wob))
+
+        def turn_out():
+            eye = (lax.broadcasted_iota(jnp.int32, (cc, cc), 0) == lax.broadcasted_iota(jnp.int32, (cc, cc), 1)).astype(F32).astype(BF16)
+            for i in range(4):
+                pair = jnp.concatenate([wob[cc * i:cc * (i + 1), :], wob[cc * (i + 4):cc * (i + 5), :]], axis=0)
+                wot[i] = lax.dot_general(eye, pair, NT, preferred_element_type=F32).astype(BF16)
+
         def load_first(l):
             return start(lc(wq_ref.at[l], wq), lc(wu_ref.at[l], wu))
 
@@ -102,6 +112,9 @@
             x2 = rc(xt.at[pl.ds(0, hs)], g.at[2, pl.ds(row, hs)], 2)
             c0 = rc(xt, g.at[1, pl.ds(row, seq)], 1)
             start(y1, x1, y2, x2, c0)
+            wl = load_out(0)
+            waitl(wl)
+            turn_out()
             y1.wait_recv()
             rx = rc(g.at[0, pl.ds(orow, hs)], g.at[2, pl.ds(orow, hs)], 2)
             rx.start()
@@ -124,33 +137,47 @@
                 return [c2, c3]
             return rest, [c0, c1]
 
-        def gather1(l):
+        def tile_cols(t, base=0):
+            off = base + t * tile
+            return pl.ds(off if isinstance(off, int) else pl.multiple_of(off, tile), tile)
+
+        def gather1(l, finish):
             g = xg_ref.at[l]
             lo, hi = pl.ds(0, seq), pl.ds(seq, seq)
-            yc, oc = pl.ds(ycol, half_d), pl.ds(ocol, half_d)
-            y1 = rc(nbuf.at[lo], g.at[0, lo, yc], 4)
-            y2 = rc(nbuf.at[hi], g.at[0, hi, yc], 4)
-            x1 = rc(nbuf.at[hi], g.at[2, hi, yc], 2)
-            x2 = rc(nbuf.at[lo], g.at[2, lo, yc], 2)
-            start(y1, x1, y2, x2)
-            own = start(lc(nbuf, g.at[0, :, yc]))
-            y1.wait_recv()
-            rx = rc(g.at[0, lo, oc], g.at[2, lo, oc], 2)
-            rx.start()
-            x1.wait_recv()
-            ry = rc(g.at[2, hi, yc], g.at[2, hi, yc], 4)
-            ry.start()
-            y2.wait_recv()
+            ys, xs, own = [], [], []
+
+            def send(t):
+                src, dc = nbuf.at[:, tile_cols(t)], tile_cols(t, ycol)
+                ys.append(rc(src, g.at[0, :, dc], 4))
+                xs.append(rc(src, g.at[2, :, dc], 2))
+                own.append(lc(src, g.at[0, :, dc]))
+                start(ys[t], xs[t], own[t])
+            for t in range(out_tiles):
+                finish(t)
+                if t:
+                    send(t - 1)
+            send(out_tiles - 1)
+            rx, ry = [], []
+            for t in range(out_tiles):
+                ys[t].wait_recv()
+                oc = tile_cols(t, ocol)
+                rx.append(rc(g.at[0, lo, oc], g.at[2, lo, oc], 2))
+                rx[t].start()
             waitl(own)
             c1 = rc(g.at[0], g.at[1], 1)
             c1.start()
-            sent.extend([y1, y2, x1, x2, rx, ry, c1])
+            sent.extend(ys + xs + rx + [c1])
 
             def rest():
-                recvs([x2, rx, ry])
+                for t in range(out_tiles):
+                    xs[t].wait_recv()
+                    yc = tile_cols(t, ycol)
+                    ry.append(rc(g.at[2, hi, yc], g.at[2, hi, yc], 4))
+                    ry[t].start()
+                recvs(rx + ry)
                 c3 = rc(g.at[2], g.at[3], 1)
                 c3.start()
-                sent.append(c3)
+                sent.extend(ry + [c3])
                 return [c3]
             return rest, [c1]
 
@@ -162,7 +189,7 @@
                 ty = flip(t, 4)
                 out.append(rc(wd_ref.at[l, :, pl.ds(pl.multiple_of(hid * t, 128), hid)], w2_ref.at[l, rows, pl.ds(0, hid)], r))
                 out.append(rc(wd_ref.at[l, :, pl.ds(pl.multiple_of(hid * ty, 128), hid)], w2_ref.at[l, rows, pl.ds(hid, hid)], r))
-                out.append(rc(wo_ref.at[l, t % 4], w2_ref.at[l, rows, pl.ds(2 * hid, 2 * cc)], r))
+                out.append(rc(wot.at[t % 4], w2_ref.at[l, rows, pl.ds(2 * hid, 2 * cc)], r))
             start(*out)
             sent.extend(out)
             return out
@@ -171,8 +198,7 @@
             rows = pl.ds(pl.multiple_of(cc * q, 64), cc)
             return start(
                 lc(wd_ref.at[l, :, pl.ds(pl.multiple_of(hid * me, 128), hid)], w2v.at[rows, pl.ds(0, hid)]),
-                lc(wd_ref.at[l, :, pl.ds(pl.multiple_of(hid * flip(me, 4), 128), hid)], w2v.at[rows, pl.ds(hid, hid)]),
-                lc(wo_ref.at[l, q], w2v.at[rows, pl.ds(2 * hid, 2 * cc)]))
+                lc(wd_ref.at[l, :, pl.ds(pl.multiple_of(hid * flip(me, 4), 128), hid)], w2v.at[rows, pl.ds(hid, hid)]))
 
         def other_weights(l, inbound):
             recvs(inbound)
@@ -188,7 +214,7 @@
             return start(lc(xg_ref.at[l, r], xbuf))
 
         def norm(l):
-            @pl.loop(0, two // 16)
+            @pl.loop(0, two // 16, unroll=4)
             def _(i):
                 rs = pl.ds(pl.multiple_of(i * 16, 16), 16)
                 v = xbuf[rs, :].astype(F32)
@@ -203,13 +229,18 @@
             cs = pl.ds(pl.multiple_of(t * tile, tile), tile)
             return rc(hbuf.at[r, :, cs], hrec_ref.at[l, r, :, cs], 4, base + t)
 
-        def up(l, r, base):
+        def up(l, r, base, now):
             @pl.loop(0, hid_tiles)
             def _(t):
                 cs = pl.ds(pl.multiple_of(t * tile, tile), tile)
                 u = jnp.dot(mbuf[...], wu[:, cs], preferred_element_type=F32)
                 hbuf[r, :, cs] = (0.5 * u * (1.0 + lax.erf(u * (0.5 ** 0.5)))).astype(BF16)
-                h_copy(l, r, t, base).start()
+
+                @pl.when((t > 0) & (t <= now))
+                def _():
+                    h_copy(l, r, t - 1, base).start()
+            if now == hid_tiles:
+                h_copy(l, r, hid_tiles - 1, base).start()
 
         def attend(l, r):
             kidx = lax.broadcasted_iota(jnp.int32, (seq, seq), 0)
@@ -240,19 +271,20 @@
                     p = (e / jnp.sum(e, axis=0, keepdims=True)).astype(BF16)
                     cbuf[r, crow, ps] = jnp.dot(vr[:, ps], p, preferred_element_type=F32).astype(BF16)
 
-        def first(l, r, prev):
+        def first(l, r, prev, now):
             xs = load_x(l, r)
             if prev:
                 waits(prev)
             waitl(xs)
             norm(l)
             base = take(hid_tiles)
-            up(l, r, base)
+            up(l, r, base, now)
             attend(l, r)
             crows = pl.ds(pl.multiple_of(cc * yb, 64), cc)
             c = rc(cbuf.at[r, crows], crec_ref.at[l, r], 4)
-            c.start()
             hcs = [h_copy(l, r, t, base) for t in range(hid_tiles)]
+            if now == hid_tiles:
+                c.start()
             return hcs, c
 
         def kv_send(l, r, ys):
@@ -286,8 +318,13 @@
                 acc = acc + lax.dot_general(cbuf[r], w2v[ts, 2 * hid:], TT, preferred_element_type=F32)
                 dst[:, ts] = acc
                 if send_to is not None:
-                    p_copy(t).start()
-            return [p_copy(t) for t in range(out_tiles)] if send_to is not None else []
+                    @pl.when(t > 0)
+                    def _():
+                        p_copy(t - 1).start()
+            if send_to is None:
+                return []
+            p_copy(out_tiles - 1).start()
+            return [p_copy(t) for t in range(out_tiles)]
 
         rest, near = gather0()
         lw = load_first(0)
@@ -301,73 +338,81 @@
             lnf[:, lo:lo + win] += lnrec[e].astype(F32)
         wait_prev = {r: [] for r in range(4)}
         p_prev = {'p2': [], 'p31': []}
-        kv_local = []
         for l in range(layers):
+            last = l + 1 == layers
             inbound = send_weights(l)
             w_own = own_weights(l)
+            w2v[pl.ds(pl.multiple_of(cc * q, 64), cc), 2 * hid:] = wot[q]
             waitl(lw)
             hc, xc = {}, {}
-            hc[0], xc[0] = first(l, 0, wait_prev[0])
+            hc[0], xc[0] = first(l, 0, wait_prev[0], HELD)
             far = rest()
-            hc[2], xc[2] = first(l, 2, wait_prev[2])
+            hc[2], xc[2] = first(l, 2, wait_prev[2], hid_tiles)
             recvs(far)
-            hc[3], xc[3] = first(l, 3, wait_prev[3])
+            hc[3], xc[3] = first(l, 3, wait_prev[3], hid_tiles)
+            start(*hc[0][HELD:], xc[0])
+            kvs = [kv_send(l, 2, 0), kv_send(l, 3, 0)]
             recvs(near)
-            hc[1], xc[1] = first(l, 1, wait_prev[1])
-            kvs = {r: [] for r in range(4)}
-            for r in range(4):
-                kvs[r].append(kv_send(l, r, 1))
-            kvs[1].append(kv_send(l, 1, 0))
-            if l + 1 < layers:
+            hc[1], xc[1] = first(l, 1, wait_prev[1], hid_tiles)
+            kvs += [kv_send(l, r, 1) for r in range(4)] + [kv_send(l, 1, 0)]
+            loc = kv_send(l, 0, 0)
+            if not last:
                 lw = load_first(l + 1)
+                lwo = load_out(l + 1)
             w_in = other_weights(l, inbound)
             waitl(w_own)
             waitl(w_in)
             second(l, 2, hc[2], xc[2], p2, None, p_prev['p2'])
             c3 = second(l, 3, hc[3], xc[3], p31, pd3, p_prev['p31'])
-            xbase = take(out_tiles)
-
-            def x_copy(t):
-                ts = pl.ds(t * tile, tile)
-                return rc(p2.at[:, ts], px.at[:, ts], 2, xbase + t)
+            xcs = []
             for t in range(out_tiles):
                 ts = slice(t * tile, (t + 1) * tile)
                 c3[t].wait_recv()
                 p2[:, ts] += pd3[:, ts]
-                x_copy(t).start()
-            xcs = [x_copy(t) for t in range(out_tiles)]
-            kvs[2].append(kv_send(l, 2, 0))
-            kvs[3].append(kv_send(l, 3, 0))
-            loc = kv_send(l, 0, 0)
+                xcs.append(rc(p2.at[:, tile_cols(t)], px.at[:, tile_cols(t)], 2))
+                if t:
+                    xcs[t - 1].start()
+            xcs[-1].start()
+            second(l, 0, hc[0], xc[0], p0, None, [])
             c1 = second(l, 1, hc[1], xc[1], p31, pd1, c3)
-            second(l, 0, hc[0], xc[0], p0, None, [])
             if l == 0:
                 waitl(res0)
-            else:
-                waits(sent)
-                sent.clear()
-            for t in range(out_tiles):
+            waits(sent)
+            sent.clear()
+            if not last:
+                waitl(lwo)
+                turn_out()
+
+            def finish(t):
                 ts = slice(t * tile, (t + 1) * tile)
                 c1[t].wait_recv()
                 xcs[t].wait_recv()
                 total = p0[:, ts] + pd1[:, ts] + px[:, ts]
                 nbuf[:, ts] = (nbuf[:, ts].astype(F32) + total).astype(BF16)
-            loc.wait()
-            if l + 1 < layers:
-                waits(sent)
-                sent.clear()
-                rest, near = gather1(l + 1)
-                wait_prev = {r: hc[r] + [xc[r]] + kvs[r] for r in range(4)}
+
+            if not last:
+                rest, near = gather1(l + 1, finish)
+                wait_prev = {r: hc[r] + [xc[r]] for r in range(4)}
+                wait_prev[0] = wait_prev[0] + kvs
                 p_prev = {'p2': xcs, 'p31': c1}
-                recvs([c for r in range(4) for c in kvs[r]])
+                loc.wait()
+                kv_in = kvs
             else:
-                fin = rc(nbuf.at[pl.ds(orow, seq)], y_ref.at[:, pl.ds(ycol, half_d)], 4)
-                fin.start()
-                loc = start(lc(nbuf.at[pl.ds(row, seq)], y_ref.at[:, pl.ds(ycol, half_d)]))
-                waits(xcs + c1 + [c for r in range(4) for c in hc[r] + [xc[r]] + kvs[r]])
-                recvs([c for r in range(4) for c in kvs[r]])
-                fin.wait()
-                waitl(loc)
+                fin, own = [], []
+
+                def send(t):
+                    dc = tile_cols(t, ycol)
+                    fin.append(rc(nbuf.at[pl.ds(orow, seq), tile_cols(t)], y_ref.at[:, dc], 4))
+                    own.append(lc(nbuf.at[pl.ds(row, seq), tile_cols(t)], y_ref.at[:, dc]))
+                    start(fin[t], own[t])
+                for t in range(out_tiles):
+                    finish(t)
+                    if t:
+                        send(t - 1)
+                send(out_tiles - 1)
+                waits(xcs + c1 + [c for r in range(4) for c in hc[r] + [xc[r]]] + kvs + fin)
+                recvs(kv_in + kvs + fin)
+                waitl(own + [loc])
         waits(lnc)
         assert counter[0] <= cfg['n_remote'] and counter[1] <= cfg['n_local'], counter
     return kernel
@@ -399,7 +444,7 @@
         ln_piece = jnp.concatenate([wide, lens, jnp.zeros((16 - 4 * layers - 1, win), BF16)], axis=0)
         wq_t = w_qkv.transpose(0, 2, 1)
         wd_t = w_down.transpose(0, 2, 1)
-        wo_t = w_out.reshape(layers, 2, 4, cc, cc).transpose(0, 2, 4, 1, 3).reshape(layers, 4, cc, 2 * cc)
+        wo_n = w_out.reshape(layers, d, -1)
 
         hbm = pl.BlockSpec(memory_space=pltpu.MemorySpace.HBM)
         vmem = pl.BlockSpec(memory_space=pltpu.MemorySpace.VMEM)
@@ -413,6 +458,7 @@
             out_specs=[hbm] * 6,
             scratch_shapes=[
                 pltpu.VMEM((3 * cc, d), BF16), pltpu.VMEM((d, hid), BF16), pltpu.VMEM((half_d, 2 * hid + 2 * cc), BF16),
+                pltpu.VMEM((d, d // n), BF16), pltpu.VMEM((4, cc, 2 * cc), BF16),
                 pltpu.VMEM((two, d), BF16), pltpu.VMEM((two, d), BF16), pltpu.VMEM((two, d), BF16),
                 pltpu.VMEM((4, two, hid), BF16), pltpu.VMEM((two, hid), BF16),
                 pltpu.VMEM((4, 2, cc, two), BF16), pltpu.VMEM((4, 2 * cc, two), BF16),
@@ -422,7 +468,7 @@
                 pltpu.SemaphoreType.DMA((cfg['n_remote'],)), pltpu.SemaphoreType.DMA((cfg['n_remote'],)),
                 pltpu.SemaphoreType.DMA((cfg['n_local'],))],
             compiler_params=pltpu.CompilerParams(collective_id=0, has_side_effects=True, vmem_limit_bytes=67043328),
-        )(x[0], wq_t, w_up, wd_t, wo_t, ln_piece, cos_t, sin_t)
+        )(x[0], wq_t, w_up, wd_t, wo_n, ln_piece, cos_t, sin_t)
         y, kv = outs[0], outs[1]
         caches = [kv[:, i].reshape(layers, 1, n_heads, hd, seq).transpose(0, 1, 4, 2, 3) for i in range(2)]
         return y[None], caches[0], caches[1]

time: 515 us -> 479 us (0.930)
  local copies, waits for them, and re-layouts: 28.9 us -> 7.9 us
  Pallas kernels: 481 us -> 467 us
    reshape x2 -> x0, local copies, waits for them, and re-layouts: 21 us -> none  [local_program(): w_out.reshape(layers, 2, 4, cc, cc).transpose(0, 2, 4, 1, 3)]
    pallas_call x1, Pallas kernels: 481 us -> 467 us  [local_program(): pl.pallas_call(make_kernel(cfg), out_shape=[sds((seq, d), BF16), sds((lay...]
where the time goes in v2:
time: 479 us
  Pallas kernels  467 us (97%)
  local copies, waits for them, and re-layouts  7.9 us (2%)
    pallas_call x1, Pallas kernels, local_program(): pl.pallas_call(make_kernel(cfg), out_shape=[sds((seq, d), BF16), sds((lay...  467 us

profile of v2, /device:TPU:0, one launch (start us, length us, event | category | flops | bytes accessed | tf_op | source)
XLA Modules:
  0.0 478.7 jit_solution(592710263061384381)
XLA Ops:
  1.3 0.1 pad.11.clone
  1.4 0.1 pad.12.clone
  1.5 0.7 convert_element_type.11
  2.1 0.7 pad_maximum_fusion
  2.9 0.1 pad_select_fusion
  3.0 0.7 maximum_maximum_fusion.ln_ref
  3.6 0.2 multiply_sine_fusion
  3.9 0.6 copy.15
  4.6 0.6 copy.14
  5.2 467.1 %shard_map.112 = (bf16[256,2560]{1,0:T(8,128)(2,1)}, bf16[2,2,2560,256]{3,2,1,0:T(8,128)(2,1)}, bf16[2,4,512,2560]{3,2,1,0:T(8,128)(2,1)}, bf16[2,1280,3200]{2,1...) custom-call(bf16[256,2560]{1,0:T(8,128)(2,1)} %bitcast.25, ...), custom_call_target="tpu_custom_call" | custom-call | tf_op jit(solution)/shard_map/pallas_call | solution.py:452
  472.3 0.0 copy-start
  472.3 5.3 %fusion = (bf16[2,1,2560,256]{3,2,1,0:T(8,128)(2,1)}, bf16[2,1,2560,256]{3,2,1,0:T(8,128)(2,1)}) fusion(bf16[2,2,2560,256]{3,2,1,0:T(8,128)(2,1)} %get-tuple-element.6), kind=kLoop, calls=%fused_computation.6 | loop fusion | bytes 10485760 | tf_op jit(solution)/shard_map/slice | solution.py:473
  477.7 0.0 copy-done
  477.7 1.1 copy.18
  (5 shorter events, 0.1 us)
Async XLA Ops:
  472.3 5.3 %copy-start = (bf16[256,2560]{1,0:T(8,128)(2,1)S(1)}, bf16[256,2560]{1,0:T(8,128)(2,1)}, u32[]{:S(2)}) copy-start(bf16[256,2560]{1,0:T(8,128)(2,1)} %get-tuple-element.5) | copy-start | bytes 3932164

commit v3 on v2

--- a/solution.py
+++ b/solution.py
@@ -13,7 +13,7 @@
 NT = (((1,), (1,)), ((), ()))
 TN = (((0,), (0,)), ((), ()))
 TT = (((0,), (1,)), ((), ()))
-HELD = 2
+HELD = 3
 
 
 def flip(v, s):
@@ -39,9 +39,9 @@
     ncols = d // n
     win = ncols + 64
 
-    def kernel(x_ref, wq_ref, wu_ref, wd_ref, wo_ref, ln_ref, cos_ref, sin_ref,
-               y_ref, kv_ref, xg_ref, w2_ref, hrec_ref, crec_ref,
-               wq, wu, w2v, wob, wot, xbuf, abuf, mbuf, hbuf, hr, kvb, cbuf, p2, p31, p0, pd3, pd1, px, nbuf, lnrec, lnf,
+    def kernel(x_ref, wq_ref, wu_ref, wd_ref, wo_ref, la_ref, lm_ref, len_ref, cos_ref, sin_ref,
+               y_ref, k_ref, v_ref, xg_ref, w2_ref, hrec_ref, crec_ref,
+               wq, wu, w2v, wob, wot, xbuf, abuf, mbuf, hbuf, hr, kvb, cbuf, p2, p31, p0, pd3, pd1, px, nbuf, lnst, lnsend, lnrec, lnf,
                ssem, rsem, lsem):
         me = lax.axis_index('wg')
         yb = me // 4
@@ -82,15 +82,23 @@
             for c in cs:
                 c.wait()
 
+        lnst[...] = jnp.zeros_like(lnst)
+        for i in range(layers):
+            lnst[4 * i:4 * i + 2, 0:ncols] = la_ref[i].astype(F32)
+            lnst[4 * i + 2:4 * i + 4, 0:ncols] = lm_ref[i].astype(F32)
+        moved = jnp.where(me % 2 == 1, pltpu.roll(lnst[...], 64, 1), lnst[...])
+        is_len = lax.broadcasted_iota(jnp.int32, (16, win), 0) == 4 * layers
+        lnsend[...] = jnp.where(is_len, len_ref[0].astype(F32), moved).astype(BF16)
+        lnrec[me] = lnsend[...]
+
         barrier = pltpu.get_barrier_semaphore()
         for s in range(1, n):
             pl.semaphore_signal(barrier, inc=1, device_id={'wg': flip(me, s)}, device_id_type=MESH)
         pl.semaphore_wait(barrier, n - 1)
 
         sent = []
-        lnc = [rc(ln_ref, lnrec.at[me], s) for s in range(1, n)]
+        lnc = [rc(lnsend, lnrec.at[me], s) for s in range(1, n)]
         start(*lnc)
-        lnl = start(lc(ln_ref, lnrec.at[me]))
 
         def load_out(l):
             return start(lc(wo_ref.at[l], wob))
@@ -113,6 +121,7 @@
             c0 = rc(xt, g.at[1, pl.ds(row, seq)], 1)
             start(y1, x1, y2, x2, c0)
             wl = load_out(0)
+            first_weights = load_first(0)
             waitl(wl)
             turn_out()
             y1.wait_recv()
@@ -135,7 +144,7 @@
                 c3.start()
                 sent.extend([c2, c3])
                 return [c2, c3]
-            return rest, [c0, c1]
+            return rest, [c0, c1], first_weights
 
         def tile_cols(t, base=0):
             off = base + t * tile
@@ -166,18 +175,18 @@
             waitl(own)
             c1 = rc(g.at[0], g.at[1], 1)
             c1.start()
-            sent.extend(ys + xs + rx + [c1])
+            for t in range(out_tiles):
+                xs[t].wait_recv()
+                yc = tile_cols(t, ycol)
+                ry.append(rc(g.at[2, hi, yc], g.at[2, hi, yc], 4))
+                ry[t].start()
+            sent.extend(ys + xs + rx + ry + [c1])
 
             def rest():
-                for t in range(out_tiles):
-                    xs[t].wait_recv()
-                    yc = tile_cols(t, ycol)
-                    ry.append(rc(g.at[2, hi, yc], g.at[2, hi, yc], 4))
-                    ry[t].start()
                 recvs(rx + ry)
                 c3 = rc(g.at[2], g.at[3], 1)
                 c3.start()
-                sent.extend(ry + [c3])
+                sent.append(c3)
                 return [c3]
             return rest, [c1]
 
@@ -252,7 +261,7 @@
             def _(h):
                 t = lax.dot_general(wq[pl.ds(pl.multiple_of(h * slot, 16), slot), :], abuf[...], NT, preferred_element_type=F32)
                 t = t.astype(BF16).astype(F32)
-                cs, sn = cos_ref[...], sin_ref[...]
+                cs, sn = (jnp.concatenate([f[...], f[...]], axis=1) for f in (cos_ref, sin_ref))
 
                 def turn(v):
                     a, b = v[:half_hd], v[half_hd:]
@@ -289,12 +298,14 @@
 
         def kv_send(l, r, ys):
             j = yb if ys == 0 else 1 - yb
-            src = kvb.at[r, :, :, pl.ds(pl.multiple_of(seq * j, seq), seq)]
-            dst = kv_ref.at[l, :, pl.ds(pl.multiple_of(cc * me, 64), cc), :]
             s = 4 * ys + r
-            c = lc(src, dst) if s == 0 else rc(src, dst, s)
-            c.start()
-            return c
+            out = []
+            for i, ref in enumerate((k_ref, v_ref)):
+                src = kvb.at[r, i, :, pl.ds(pl.multiple_of(seq * j, seq), seq)]
+                dst = ref.at[l, pl.ds(pl.multiple_of(cc * me, 64), cc), :]
+                out.append(lc(src, dst) if s == 0 else rc(src, dst, s))
+            start(*out)
+            return out
 
         def second(l, r, hcs, c, dst, send_to, wait_before):
             recvs(hcs)
@@ -326,12 +337,10 @@
             p_copy(out_tiles - 1).start()
             return [p_copy(t) for t in range(out_tiles)]
 
-        rest, near = gather0()
-        lw = load_first(0)
+        rest, near, lw = gather0()
         res0 = start(lc(x_ref.at[:, pl.ds(ycol, half_d)], nbuf.at[pl.ds(row, seq)]),
                      lc(xg_ref.at[0, 0, pl.ds(orow, seq), pl.ds(ycol, half_d)], nbuf.at[pl.ds(orow, seq)]))
         recvs(lnc)
-        waitl(lnl)
         lnf[...] = jnp.zeros_like(lnf)
         for e in range(n):
             lo = ncols * e - 64 * (e % 2)
@@ -351,10 +360,12 @@
             recvs(far)
             hc[3], xc[3] = first(l, 3, wait_prev[3], hid_tiles)
             start(*hc[0][HELD:], xc[0])
-            kvs = [kv_send(l, 2, 0), kv_send(l, 3, 0)]
+            kvs = kv_send(l, 2, 0) + kv_send(l, 3, 0) + (kv_send(l, 2, 1) if last else [])
             recvs(near)
             hc[1], xc[1] = first(l, 1, wait_prev[1], hid_tiles)
-            kvs += [kv_send(l, r, 1) for r in range(4)] + [kv_send(l, 1, 0)]
+            for r in range(2 if last else 4):
+                kvs += kv_send(l, r, 1)
+            kvs += kv_send(l, 1, 0)
             loc = kv_send(l, 0, 0)
             if not last:
                 lw = load_first(l + 1)
@@ -395,7 +406,7 @@
                 wait_prev = {r: hc[r] + [xc[r]] for r in range(4)}
                 wait_prev[0] = wait_prev[0] + kvs
                 p_prev = {'p2': xcs, 'p31': c1}
-                loc.wait()
+                waitl(loc)
                 kv_in = kvs
             else:
                 fin, own = [], []
@@ -410,9 +421,10 @@
                     if t:
                         send(t - 1)
                 send(out_tiles - 1)
+                kvs += kv_send(l, 3, 1)
                 waits(xcs + c1 + [c for r in range(4) for c in hc[r] + [xc[r]]] + kvs + fin)
                 recvs(kv_in + kvs + fin)
-                waitl(own + [loc])
+                waitl(own + loc)
         waits(lnc)
         assert counter[0] <= cfg['n_remote'] and counter[1] <= cfg['n_local'], counter
     return kernel
@@ -436,12 +448,8 @@
         half_hd = hd // 2
         inv_freq = ROPE_BASE ** (-jnp.arange(half_hd, dtype=F32) * 2.0 / hd)
         angles = positions.astype(F32)[None, :] * inv_freq[:, None]
-        cos_t, sin_t = (jnp.tile(f(angles), (1, 2)) for f in (jnp.cos, jnp.sin))
-        ln = jnp.concatenate([ln_attn, ln_mlp], axis=1).reshape(4 * layers, -1)
-        wide = jnp.where(me % 2 == 1, jnp.pad(ln, ((0, 0), (64, 0))), jnp.pad(ln, ((0, 0), (0, 64))))
-        win = wide.shape[1]
-        lens = jnp.broadcast_to(prompt_len.astype(BF16)[:, None], (1, win))
-        ln_piece = jnp.concatenate([wide, lens, jnp.zeros((16 - 4 * layers - 1, win), BF16)], axis=0)
+        cos_t, sin_t = jnp.cos(angles), jnp.sin(angles)
+        win = d // n + 64
         wq_t = w_qkv.transpose(0, 2, 1)
         wd_t = w_down.transpose(0, 2, 1)
         wo_n = w_out.reshape(layers, d, -1)
@@ -452,10 +460,10 @@
         outs = pl.pallas_call(
             make_kernel(cfg),
             out_shape=[
-                sds((seq, d), BF16), sds((layers, 2, d, seq), BF16), sds((layers, 4, two, d), BF16),
+                sds((seq, d), BF16), sds((layers, d, seq), BF16), sds((layers, d, seq), BF16), sds((layers, 4, two, d), BF16),
                 sds((layers, half_d, 2 * hid + 2 * cc), BF16), sds((layers, 4, two, hid), BF16), sds((layers, 4, cc, two), BF16)],
-            in_specs=[hbm] * 5 + [hbm, vmem, vmem],
-            out_specs=[hbm] * 6,
+            in_specs=[hbm] * 5 + [vmem, vmem, pl.BlockSpec(memory_space=pltpu.MemorySpace.SMEM), vmem, vmem],
+            out_specs=[hbm] * 7,
             scratch_shapes=[
                 pltpu.VMEM((3 * cc, d), BF16), pltpu.VMEM((d, hid), BF16), pltpu.VMEM((half_d, 2 * hid + 2 * cc), BF16),
                 pltpu.VMEM((d, d // n), BF16), pltpu.VMEM((4, cc, 2 * cc), BF16),
@@ -464,13 +472,12 @@
                 pltpu.VMEM((4, 2, cc, two), BF16), pltpu.VMEM((4, 2 * cc, two), BF16),
                 pltpu.VMEM((two, half_d), F32), pltpu.VMEM((two, half_d), F32), pltpu.VMEM((two, half_d), F32),
                 pltpu.VMEM((two, half_d), F32), pltpu.VMEM((two, half_d), F32), pltpu.VMEM((two, half_d), F32),
-                pltpu.VMEM((two, half_d), BF16), pltpu.VMEM((n, 16, win), BF16), pltpu.VMEM((16, d), F32),
+                pltpu.VMEM((two, half_d), BF16), pltpu.VMEM((16, win), F32), pltpu.VMEM((16, win), BF16), pltpu.VMEM((n, 16, win), BF16), pltpu.VMEM((16, d), F32),
                 pltpu.SemaphoreType.DMA((cfg['n_remote'],)), pltpu.SemaphoreType.DMA((cfg['n_remote'],)),
                 pltpu.SemaphoreType.DMA((cfg['n_local'],))],
             compiler_params=pltpu.CompilerParams(collective_id=0, has_side_effects=True, vmem_limit_bytes=67043328),
-        )(x[0], wq_t, w_up, wd_t, wo_n, ln_piece, cos_t, sin_t)
-        y, kv = outs[0], outs[1]
-        caches = [kv[:, i].reshape(layers, 1, n_heads, hd, seq).transpose(0, 1, 4, 2, 3) for i in range(2)]
-        return y[None], caches[0], caches[1]
+        )(x[0], wq_t, w_up, wd_t, wo_n, ln_attn, ln_mlp, prompt_len, cos_t, sin_t)
+        caches = [c.reshape(layers, 1, n_heads, hd, seq).transpose(0, 1, 4, 2, 3) for c in outs[1:3]]
+        return outs[0][None], caches[0], caches[1]
 
     return jax.shard_map(local_program, mesh=mesh, in_specs=(batch_spec, P('dp'), batch_spec, col_spec, col_spec, col_spec, out_spec, col_spec, col_spec), out_specs=(batch_spec, cache_spec, cache_spec), check_vma=False)

time: 479 us -> 460 us (0.960)
  Pallas kernels: 467 us -> 450 us
    pallas_call x1, Pallas kernels: 467 us -> 450 us  [local_program(): pl.pallas_call(make_kernel(cfg), out_shape=[sds((seq, d), BF16), sds((lay...]
    slice x1 -> x0, local copies, waits for them, and re-layouts: 5.33 us -> none  [local_program(): kv[:, i].reshape(layers, 1, n_heads, hd, seq).transpose(0, 1, 4, 2, 3)]
where the time goes in v3:
time: 460 us; the launch traced here: 459 us
  Pallas kernels  450 us (98%)
  local copies, waits for them, and re-layouts  6.79 us (1%)
    pallas_call x1, Pallas kernels, local_program(): pl.pallas_call(make_kernel(cfg), out_shape=[sds((seq, d), BF16), sds((lay...  450 us

profile of v3, /device:TPU:0, one launch (start us, length us, event | category | flops | bytes accessed | tf_op | source)
XLA Modules:
  0.0 459.3 jit_solution(8161189700130656035)
XLA Ops:
  1.3 0.7 convert_element_type.3
  2.0 0.9 multiply_sine_fusion
  2.8 449.6 %shard_map.112 = (bf16[256,2560]{1,0:T(8,128)(2,1)}, bf16[2,2560,256]{2,1,0:T(8,128)(2,1)}, bf16[2,2560,256]{2,1,0:T(8,128)(2,1)}, bf16[2,4,512,2560]{3,2,1,0:T(...) custom-call(bf16[256,2560]{1,0:T(8,128)(2,1)} %bitcast.20, ...), custom_call_target="tpu_custom_call" | custom-call | tf_op jit(solution)/shard_map/pallas_call | solution.py:460
  452.5 0.0 copy-start.1
  452.5 2.6 copy.18
  455.1 0.0 copy-done.1
  455.1 0.0 copy-start
  455.1 1.5 copy.19
  456.6 1.2 copy-done
  457.8 1.5 copy.20
  (1 shorter events, 0.0 us)
Async XLA Ops:
  452.5 2.6 copy-start.1
  455.1 2.7 copy-start

commit v4 on v3

--- a/solution.py
+++ b/solution.py
@@ -1,5 +1,6 @@
 import jax
 import jax.numpy as jnp
+import numpy as np
 from jax import lax
 from jax.experimental import pallas as pl
 from jax.experimental.pallas import tpu as pltpu
@@ -31,7 +32,8 @@
     two = 2 * seq
     cc = heads * hd
     half_d = d // 2
-    hs = seq // 2
+    hs = 112
+    ht = seq - hs
     slot = 3 * hd
     half_hd = hd // 2
     tile = 256
@@ -39,9 +41,9 @@
     ncols = d // n
     win = ncols + 64
 
-    def kernel(x_ref, wq_ref, wu_ref, wd_ref, wo_ref, la_ref, lm_ref, len_ref, cos_ref, sin_ref,
+    def kernel(x_ref, wq_ref, wu_ref, wd_ref, wo_ref, la_ref, lm_ref, len_ref, pos_ref, freq_ref,
                y_ref, k_ref, v_ref, xg_ref, w2_ref, hrec_ref, crec_ref,
-               wq, wu, w2v, wob, wot, xbuf, abuf, mbuf, hbuf, hr, kvb, cbuf, p2, p31, p0, pd3, pd1, px, nbuf, lnst, lnsend, lnrec, lnf,
+               wq, wu, w2v, wob, wot, xbuf, abuf, mbuf, hbuf, hr, kvb, cbuf, p2, p31, p0, pd3, pd1, px, nbuf, cos_ref, sin_ref, lnst, lnsend, lnrec, lnf,
                ssem, rsem, lsem):
         me = lax.axis_index('wg')
         yb = me // 4
@@ -82,6 +84,15 @@
             for c in cs:
                 c.wait()
 
+        barrier = pltpu.get_barrier_semaphore()
+        for s in range(1, n):
+            pl.semaphore_signal(barrier, inc=1, device_id={'wg': flip(me, s)}, device_id_type=MESH)
+
+        angles = freq_ref[...] * pos_ref[...].astype(F32)
+        for f, ref in ((jnp.cos, cos_ref), (jnp.sin, sin_ref)):
+            ref[:, 0:seq] = f(angles)
+            ref[:, seq:two] = ref[:, 0:seq]
+
         lnst[...] = jnp.zeros_like(lnst)
         for i in range(layers):
             lnst[4 * i:4 * i + 2, 0:ncols] = la_ref[i].astype(F32)
@@ -90,15 +101,10 @@
         is_len = lax.broadcasted_iota(jnp.int32, (16, win), 0) == 4 * layers
         lnsend[...] = jnp.where(is_len, len_ref[0].astype(F32), moved).astype(BF16)
         lnrec[me] = lnsend[...]
-
-        barrier = pltpu.get_barrier_semaphore()
-        for s in range(1, n):
-            pl.semaphore_signal(barrier, inc=1, device_id={'wg': flip(me, s)}, device_id_type=MESH)
         pl.semaphore_wait(barrier, n - 1)
 
         sent = []
         lnc = [rc(lnsend, lnrec.at[me], s) for s in range(1, n)]
-        start(*lnc)
 
         def load_out(l):
             return start(lc(wo_ref.at[l], wob))
@@ -115,11 +121,11 @@
         def gather0():
             xt, g = x_ref, xg_ref.at[0]
             y1 = rc(xt.at[pl.ds(0, hs)], g.at[0, pl.ds(row, hs)], 4)
-            y2 = rc(xt.at[pl.ds(hs, hs)], g.at[0, pl.ds(row + hs, hs)], 4)
-            x1 = rc(xt.at[pl.ds(hs, hs)], g.at[2, pl.ds(row + hs, hs)], 2)
+            y2 = rc(xt.at[pl.ds(hs, ht)], g.at[0, pl.ds(row + hs, ht)], 4)
+            x1 = rc(xt.at[pl.ds(hs, ht)], g.at[2, pl.ds(row + hs, ht)], 2)
             x2 = rc(xt.at[pl.ds(0, hs)], g.at[2, pl.ds(row, hs)], 2)
             c0 = rc(xt, g.at[1, pl.ds(row, seq)], 1)
-            start(y1, x1, y2, x2, c0)
+            start(y1, x1, y2, x2, c0, *lnc)
             wl = load_out(0)
             first_weights = load_first(0)
             waitl(wl)
@@ -128,7 +134,7 @@
             rx = rc(g.at[0, pl.ds(orow, hs)], g.at[2, pl.ds(orow, hs)], 2)
             rx.start()
             x1.wait_recv()
-            ry = rc(g.at[2, pl.ds(row + hs, hs)], g.at[2, pl.ds(row + hs, hs)], 4)
+            ry = rc(g.at[2, pl.ds(row + hs, ht)], g.at[2, pl.ds(row + hs, ht)], 4)
             ry.start()
             y2.wait_recv()
             c1 = rc(g.at[0, pl.ds(orow, seq)], g.at[1, pl.ds(orow, seq)], 1)
@@ -152,7 +158,7 @@
 
         def gather1(l, finish):
             g = xg_ref.at[l]
-            lo, hi = pl.ds(0, seq), pl.ds(seq, seq)
+            lo, hi = pl.ds(0, 304), pl.ds(304, two - 304)
             ys, xs, own = [], [], []
 
             def send(t):
@@ -261,7 +267,7 @@
             def _(h):
                 t = lax.dot_general(wq[pl.ds(pl.multiple_of(h * slot, 16), slot), :], abuf[...], NT, preferred_element_type=F32)
                 t = t.astype(BF16).astype(F32)
-                cs, sn = (jnp.concatenate([f[...], f[...]], axis=1) for f in (cos_ref, sin_ref))
+                cs, sn = cos_ref[...], sin_ref[...]
 
                 def turn(v):
                     a, b = v[:half_hd], v[half_hd:]
@@ -446,9 +452,8 @@
         me = lax.axis_index('wg')
         cfg = dict(n=n, layers=layers, seq=seq, d=d, heads=heads, hd=hd, hid=hid, n_remote=192, n_local=96)
         half_hd = hd // 2
-        inv_freq = ROPE_BASE ** (-jnp.arange(half_hd, dtype=F32) * 2.0 / hd)
-        angles = positions.astype(F32)[None, :] * inv_freq[:, None]
-        cos_t, sin_t = jnp.cos(angles), jnp.sin(angles)
+        inv_freq = (ROPE_BASE ** (-np.arange(half_hd) * 2.0 / hd)).astype(np.float32)
+        freq = jnp.asarray(inv_freq[:, None])
         win = d // n + 64
         wq_t = w_qkv.transpose(0, 2, 1)
         wd_t = w_down.transpose(0, 2, 1)
@@ -472,11 +477,11 @@
                 pltpu.VMEM((4, 2, cc, two), BF16), pltpu.VMEM((4, 2 * cc, two), BF16),
                 pltpu.VMEM((two, half_d), F32), pltpu.VMEM((two, half_d), F32), pltpu.VMEM((two, half_d), F32),
                 pltpu.VMEM((two, half_d), F32), pltpu.VMEM((two, half_d), F32), pltpu.VMEM((two, half_d), F32),
-                pltpu.VMEM((two, half_d), BF16), pltpu.VMEM((16, win), F32), pltpu.VMEM((16, win), BF16), pltpu.VMEM((n, 16, win), BF16), pltpu.VMEM((16, d), F32),
+                pltpu.VMEM((two, half_d), BF16), pltpu.VMEM((half_hd, two), F32), pltpu.VMEM((half_hd, two), F32), pltpu.VMEM((16, win), F32), pltpu.VMEM((16, win), BF16), pltpu.VMEM((n, 16, win), BF16), pltpu.VMEM((16, d), F32),
                 pltpu.SemaphoreType.DMA((cfg['n_remote'],)), pltpu.SemaphoreType.DMA((cfg['n_remote'],)),
                 pltpu.SemaphoreType.DMA((cfg['n_local'],))],
             compiler_params=pltpu.CompilerParams(collective_id=0, has_side_effects=True, vmem_limit_bytes=67043328),
-        )(x[0], wq_t, w_up, wd_t, wo_n, ln_attn, ln_mlp, prompt_len, cos_t, sin_t)
+        )(x[0], wq_t, w_up, wd_t, wo_n, ln_attn, ln_mlp, prompt_len, positions[None, :], freq)
         caches = [c.reshape(layers, 1, n_heads, hd, seq).transpose(0, 1, 4, 2, 3) for c in outs[1:3]]
         return outs[0][None], caches[0], caches[1]
 

time: 460 us -> 457 us (level)
  no operation moved by 1% of the time
where the time goes in v4:
time: 457 us; the launch traced here: 456 us
  Pallas kernels  448 us (98%)
  local copies, waits for them, and re-layouts  6.79 us (1%)
    pallas_call x1, Pallas kernels, local_program(): pl.pallas_call(make_kernel(cfg), out_shape=[sds((seq, d), BF16), sds((lay...  448 us

profile of v4, /device:TPU:0, one launch (start us, length us, event | category | flops | bytes accessed | tf_op | source)
XLA Modules:
  0.0 456.4 jit_solution(71123667914982272)
XLA Ops:
  1.3 448.3 %shard_map.121 = (bf16[256,2560]{1,0:T(8,128)(2,1)}, bf16[2,2560,256]{2,1,0:T(8,128)(2,1)}, bf16[2,2560,256]{2,1,0:T(8,128)(2,1)}, bf16[2,4,512,2560]{3,2,1,0:T(...) custom-call(bf16[256,2560]{1,0:T(8,128)(2,1)} %bitcast.21, ...), custom_call_target="tpu_custom_call" | custom-call | tf_op jit(solution)/shard_map/pallas_call | solution.py:465
  449.6 0.0 copy-start.1
  449.6 2.6 copy.19
  452.2 0.0 copy-done.1
  452.2 0.0 copy-start
  452.2 1.5 copy.20
  453.7 1.2 copy-done
  454.9 1.5 copy.21
Async XLA Ops:
  449.6 2.6 copy-start.1
  452.2 2.7 copy-start

commit v5 on v4

--- a/solution.py
+++ b/solution.py
@@ -436,6 +436,37 @@
     return kernel
 
 
+def hand_over(parts):
+    def kernel(*refs):
+        srcs, dsts = refs[:3], refs[3:6]
+        bufs, rsem, wsem = refs[6:9], refs[9], refs[10]
+        pieces = []
+        for a in range(3):
+            rows = srcs[a].shape[0] // parts[a]
+            for i in range(parts[a]):
+                pieces.append((a, pl.ds(i * rows, rows)))
+        reads = [pltpu.make_async_copy(srcs[a].at[rs], bufs[a].at[rs], rsem.at[i]) for i, (a, rs) in enumerate(pieces)]
+        writes = [pltpu.make_async_copy(bufs[a].at[rs], dsts[a].at[rs], wsem.at[i]) for i, (a, rs) in enumerate(pieces)]
+        for c in reads:
+            c.start()
+        for r, w in zip(reads, writes):
+            r.wait()
+            w.start()
+        for w in writes:
+            w.wait()
+
+    def call(*arrays):
+        hbm = pl.BlockSpec(memory_space=pltpu.MemorySpace.HBM)
+        total = sum(parts)
+        return pl.pallas_call(
+            kernel,
+            out_shape=[jax.ShapeDtypeStruct(a.shape, a.dtype) for a in arrays],
+            in_specs=[hbm] * 3, out_specs=[hbm] * 3,
+            scratch_shapes=[pltpu.VMEM(a.shape, a.dtype) for a in arrays] + [pltpu.SemaphoreType.DMA((total,)), pltpu.SemaphoreType.DMA((total,))],
+        )(*arrays)
+    return call
+
+
 def solution(mesh):
     n = mesh.shape['wg']
     batch_spec = P(('dp', 'wg'))
@@ -482,7 +513,8 @@
                 pltpu.SemaphoreType.DMA((cfg['n_local'],))],
             compiler_params=pltpu.CompilerParams(collective_id=0, has_side_effects=True, vmem_limit_bytes=67043328),
         )(x[0], wq_t, w_up, wd_t, wo_n, ln_attn, ln_mlp, prompt_len, positions[None, :], freq)
-        caches = [c.reshape(layers, 1, n_heads, hd, seq).transpose(0, 1, 4, 2, 3) for c in outs[1:3]]
-        return outs[0][None], caches[0], caches[1]
+        y, kc, vc = hand_over((2, 4, 4))(outs[0], outs[1].reshape(layers * d, seq), outs[2].reshape(layers * d, seq))
+        caches = [c.reshape(layers, 1, n_heads, hd, seq).transpose(0, 1, 4, 2, 3) for c in (kc, vc)]
+        return y[None], caches[0], caches[1]
 
     return jax.shard_map(local_program, mesh=mesh, in_specs=(batch_spec, P('dp'), batch_spec, col_spec, col_spec, col_spec, out_spec, col_spec, col_spec), out_specs=(batch_spec, cache_spec, cache_spec), check_vma=False)

time: 457 us -> 456 us (level)
  local copies, waits for them, and re-layouts: 6.79 us -> 0 us
  Pallas kernels: 448 us -> 454 us
    unnamed x7 -> x0, local copies, waits for them, and re-layouts: 6.79 us -> none
    pallas_call x0 -> x1, Pallas kernels: none -> 5.53 us  [call(): pl.pallas_call(kernel, out_shape=[jax.ShapeDtypeStruct(a.shape, a.dtype)...]
where the time goes in v5:
time: 456 us; the launch traced here: 455 us
  Pallas kernels  454 us (100%)
    pallas_call x1, Pallas kernels, local_program(): pl.pallas_call(make_kernel(cfg), out_shape=[sds((seq, d), BF16), sds((lay...  448 us

profile of v5, /device:TPU:0, one launch (start us, length us, event | category | flops | bytes accessed | tf_op | source)
XLA Modules:
  0.0 455.3 jit_solution(5937494611410607573)
XLA Ops:
  1.3 448.3 %shard_map.121 = (bf16[256,2560]{1,0:T(8,128)(2,1)}, bf16[2,2560,256]{2,1,0:T(8,128)(2,1)}, bf16[2,2560,256]{2,1,0:T(8,128)(2,1)}, bf16[2,4,512,2560]{3,2,1,0:T(...) custom-call(bf16[256,2560]{1,0:T(8,128)(2,1)} %bitcast.23, ...), custom_call_target="tpu_custom_call" | custom-call | tf_op jit(solution)/shard_map/pallas_call | solution.py:496
  449.6 5.5 %shard_map.122 = (bf16[256,2560]{1,0:T(8,128)(2,1)}, bf16[5120,256]{1,0:T(8,128)(2,1)}, bf16[5120,256]{1,0:T(8,128)(2,1)}) custom-call(bf16[256,2560]{1,0:T(8,128)(2,1)} %get-tuple-element.9.refs_0_, bf16[5120,256]{1,0:T(8,128)(2,1)} %bitcast.21, bf16[5120,256]{1,0:T(8,128)(2,1)} %bitcast.22), custom_call_target="tpu_custom_call" | custom-call | tf_op jit(solution)/shard_map/pallas_call | solution.py:461

commit v6 on v5

--- a/solution.py
+++ b/solution.py
@@ -274,8 +274,8 @@
                     return jnp.concatenate([a * cs - b * sn, b * cs + a * sn], axis=0).astype(BF16)
                 qr, kr, vr = turn(t[:hd]), turn(t[hd:2 * hd]), t[2 * hd:].astype(BF16)
                 hrow = pl.ds(pl.multiple_of(h * hd, 16), hd)
-                kvb[r, 0, hrow, :] = kr
-                kvb[r, 1, hrow, :] = vr
+                kvb[4 * l + r, 0, hrow, :] = kr
+                kvb[4 * l + r, 1, hrow, :] = vr
                 crow = pl.ds(pl.multiple_of(cc * yb + h * hd, 16), hd)
                 for j in range(2):
                     ps = slice(j * seq, (j + 1) * seq)
@@ -307,7 +307,7 @@
             s = 4 * ys + r
             out = []
             for i, ref in enumerate((k_ref, v_ref)):
-                src = kvb.at[r, i, :, pl.ds(pl.multiple_of(seq * j, seq), seq)]
+                src = kvb.at[4 * l + r, i, :, pl.ds(pl.multiple_of(seq * j, seq), seq)]
                 dst = ref.at[l, pl.ds(pl.multiple_of(cc * me, 64), cc), :]
                 out.append(lc(src, dst) if s == 0 else rc(src, dst, s))
             start(*out)
@@ -356,6 +356,10 @@
         for l in range(layers):
             last = l + 1 == layers
             inbound = send_weights(l)
+            late = []
+            if l:
+                for r in (2, 3):
+                    late += kv_send(l - 1, r, 1)
             w_own = own_weights(l)
             w2v[pl.ds(pl.multiple_of(cc * q, 64), cc), 2 * hid:] = wot[q]
             waitl(lw)
@@ -369,7 +373,7 @@
             kvs = kv_send(l, 2, 0) + kv_send(l, 3, 0) + (kv_send(l, 2, 1) if last else [])
             recvs(near)
             hc[1], xc[1] = first(l, 1, wait_prev[1], hid_tiles)
-            for r in range(2 if last else 4):
+            for r in range(2):
                 kvs += kv_send(l, r, 1)
             kvs += kv_send(l, 1, 0)
             loc = kv_send(l, 0, 0)
@@ -410,7 +414,6 @@
             if not last:
                 rest, near = gather1(l + 1, finish)
                 wait_prev = {r: hc[r] + [xc[r]] for r in range(4)}
-                wait_prev[0] = wait_prev[0] + kvs
                 p_prev = {'p2': xcs, 'p31': c1}
                 waitl(loc)
                 kv_in = kvs
@@ -428,8 +431,9 @@
                         send(t - 1)
                 send(out_tiles - 1)
                 kvs += kv_send(l, 3, 1)
+                kvs += kv_in + late
                 waits(xcs + c1 + [c for r in range(4) for c in hc[r] + [xc[r]]] + kvs + fin)
-                recvs(kv_in + kvs + fin)
+                recvs(kvs + fin)
                 waitl(own + loc)
         waits(lnc)
         assert counter[0] <= cfg['n_remote'] and counter[1] <= cfg['n_local'], counter
@@ -505,7 +509,7 @@
                 pltpu.VMEM((d, d // n), BF16), pltpu.VMEM((4, cc, 2 * cc), BF16),
                 pltpu.VMEM((two, d), BF16), pltpu.VMEM((two, d), BF16), pltpu.VMEM((two, d), BF16),
                 pltpu.VMEM((4, two, hid), BF16), pltpu.VMEM((two, hid), BF16),
-                pltpu.VMEM((4, 2, cc, two), BF16), pltpu.VMEM((4, 2 * cc, two), BF16),
+                pltpu.VMEM((4 * layers, 2, cc, two), BF16), pltpu.VMEM((4, 2 * cc, two), BF16),
                 pltpu.VMEM((two, half_d), F32), pltpu.VMEM((two, half_d), F32), pltpu.VMEM((two, half_d), F32),
                 pltpu.VMEM((two, half_d), F32), pltpu.VMEM((two, half_d), F32), pltpu.VMEM((two, half_d), F32),
                 pltpu.VMEM((two, half_d), BF16), pltpu.VMEM((half_hd, two), F32), pltpu.VMEM((half_hd, two), F32), pltpu.VMEM((16, win), F32), pltpu.VMEM((16, win), BF16), pltpu.VMEM((n, 16, win), BF16), pltpu.VMEM((16, d), F32),

time: 456 us -> 461 us (1.011)
  Pallas kernels: 454 us -> 459 us
    pallas_call x1, Pallas kernels: 448 us -> 454 us  [local_program(): pl.pallas_call(make_kernel(cfg), out_shape=[sds((seq, d), BF16), sds((lay...]
where the time goes in v6:
time: 461 us
  Pallas kernels  459 us (100%)
    pallas_call x1, Pallas kernels, local_program(): pl.pallas_call(make_kernel(cfg), out_shape=[sds((seq, d), BF16), sds((lay...  454 us

profile of v6, /device:TPU:0, one launch (start us, length us, event | category | flops | bytes accessed | tf_op | source)
XLA Modules:
  0.0 460.5 jit_solution(6199763398144750086)
XLA Ops:
  1.3 453.5 %shard_map.121 = (bf16[256,2560]{1,0:T(8,128)(2,1)}, bf16[2,2560,256]{2,1,0:T(8,128)(2,1)}, bf16[2,2560,256]{2,1,0:T(8,128)(2,1)}, bf16[2,4,512,2560]{3,2,1,0:T(...) custom-call(bf16[256,2560]{1,0:T(8,128)(2,1)} %bitcast.23, ...), custom_call_target="tpu_custom_call" | custom-call | tf_op jit(solution)/shard_map/pallas_call | solution.py:500
  454.8 5.5 %shard_map.122 = (bf16[256,2560]{1,0:T(8,128)(2,1)}, bf16[5120,256]{1,0:T(8,128)(2,1)}, bf16[5120,256]{1,0:T(8,128)(2,1)}) custom-call(bf16[256,2560]{1,0:T(8,128)(2,1)} %get-tuple-element.9.refs_0_, bf16[5120,256]{1,0:T(8,128)(2,1)} %bitcast.21, bf16[5120,256]{1,0:T(8,128)(2,1)} %bitcast.22), custom_call_target="tpu_custom_call" | custom-call | tf_op jit(solution)/shard_map/pallas_call | solution.py:465
